TPU v7x, 256 devices: a whole 4x4x8 slice. The times are simulated.
256 devices in a mesh: gx: 8 (over z), gy: 8 (over y, core), gz: 4 (over x).
Axes of the slice: x: 4, y: 4, z: 8, core: 2. Of those that a mesh axis runs over, the one named last changes fastest.
Arguments:
- density: float32 [64, 64, 512], P('gx', 'gy', 'gz'), may hold values from 0.5 to 2
- base_velocity: float32 [3, 64, 64, 512], P(None, 'gx', 'gy', 'gz'), may hold values from -0.4 to 0.4
- cells: int32 [3, 65536], P(None, ('gx', 'gy', 'gz')), may hold values from 0 to 511, as said below
- offsets: float32 [3, 65536], P(None, ('gx', 'gy', 'gz')), may hold values from 0 to 1
- target: float32 [3, 65536], P(None, ('gx', 'gy', 'gz')), may hold values from -0.4 to 0.4
- stiffness: float32 [65536], P(('gx', 'gy', 'gz')), may hold values from 0.01 to 0.1
- counts: int32 [256], P(('gx', 'gy', 'gz')), may hold values from 1 to 256, as said below
Outputs:
- forces: float32 [3, 65536], P(None, ('gx', 'gy', 'gz'))
Inputs may be any that keep to these rules, and one draw needn't show every extreme that they name: `cells`: each marker's cell lies inside the lattice block of the device that holds its slot. `counts`: some device holds exactly 256 live markers in every draw.
All inputs are finite; a program needn't handle non-finite values.
Results may differ from a plain program's by a relative error of at most 0.0001.
Values sent between devices are 32-bit elements; how exact they have to be, the bound alone decides.
A program may use at most 64 MiB of HBM per device.

v0:
```python
import jax
import jax.numpy as jnp
from jax import lax
from jax.sharding import Mesh
from jax.sharding import PartitionSpec as P

ITERS = 3
GY = ("gy_0", "gy_1")
GX_GY_GZ = ("gx", "gy_0", "gy_1", "gz")


def shifted(shard, axis, by):
    length = lax.axis_size(axis)
    return lax.ppermute(shard, axis, [(i, (i + by) % length) for i in range(length)])


def extended(cells, sides, width):
    for axis, dim in sides:
        count = lax.axis_size(axis)
        head = lax.slice_in_dim(cells, 0, width, axis=dim)
        tail = lax.slice_in_dim(cells, cells.shape[dim] - width, cells.shape[dim], axis=dim)
        cells = jnp.concatenate(
            [
                lax.ppermute(tail, axis, [(i, (i + 1) % count) for i in range(count)]),
                cells,
                lax.ppermute(head, axis, [((i + 1) % count, i) for i in range(count)]),
            ],
            axis=dim,
        )
    return cells


def one_axis_at_a_time(shard, axes):
    for axis in axes:
        shard = lax.psum(shard, axis)
    return shard


def moving_directions():
    listing = []
    for along_x in (-1, 0, 1):
        for along_y in (-1, 0, 1):
            for along_z in (-1, 0, 1):
                order = abs(along_x) + abs(along_y) + abs(along_z)
                if order == 1:
                    listing.append((along_x, along_y, along_z, 1.0 / 18.0))
                elif order == 2:
                    listing.append((along_x, along_y, along_z, 1.0 / 36.0))
    return listing


def delta_weights(fraction):

    def inner(radius):
        return (3.0 - 2.0 * radius + jnp.sqrt(1.0 + 4.0 * radius - 4.0 * radius * radius)) / 8.0

    def outer(radius):
        return (5.0 - 2.0 * radius - jnp.sqrt(-7.0 + 12.0 * radius - 4.0 * radius * radius)) / 8.0

    return jnp.stack(
        [outer(1.0 + fraction), inner(fraction), inner(1.0 - fraction), outer(2.0 - fraction)]
    )


def axis_rows(local, fraction, offset, extent):
    places = local[None, :] + jnp.arange(4, dtype=jnp.int32)[:, None] + offset
    hits = (places[:, :, None] == jnp.arange(extent, dtype=jnp.int32)[None, None, :]).astype(
        jnp.float32
    )
    return jnp.sum(delta_weights(fraction)[:, :, None] * hits, axis=0)


def make_tables(local, fractions, offset, extents):
    table_x = axis_rows(local[0], fractions[0], offset, extents[0]).T
    table_y = axis_rows(local[1], fractions[1], offset, extents[1]).T
    table_z = axis_rows(local[2], fractions[2], offset, extents[2])
    return (table_x, table_y, table_z)


def spread_dense(vector, tables):
    table_x, table_y, table_z = tables
    weighted = vector[:, None, None, :] * table_x[None, :, None, :] * table_y[None, None, :, :]
    return jnp.einsum("cxym,mz->cxyz", weighted, table_z, precision=lax.Precision.HIGHEST)


def interpolate_dense(field, tables):
    table_x, table_y, table_z = tables
    partial_rows = jnp.einsum("cxyz,mz->cxym", field, table_z, precision=lax.Precision.HIGHEST)
    return jnp.sum(partial_rows * (table_x[:, None, :] * table_y[None, :, :])[None], axis=(1, 2))


def surround(payload):
    stack = payload[None]
    tags = [(0, 0, 0)]
    pieces = [stack]
    grown = list(tags)
    for by in (-1, 1):
        pieces.append(shifted(stack, "gx", by))
        grown = grown + [(by, tag[1], tag[2]) for tag in tags]
    stack = jnp.concatenate(pieces, axis=0)
    tags = grown
    pieces = [stack]
    for by in (-1, 1):
        pieces.append(shifted(stack, GY, by))
        grown = grown + [(tag[0], by, tag[2]) for tag in tags]
    stack = jnp.concatenate(pieces, axis=0)
    tags = grown
    pieces = [stack]
    for by in (-1, 1):
        pieces.append(shifted(stack, "gz", by))
        grown = grown + [(tag[0], tag[1], by) for tag in tags]
    stack = jnp.concatenate(pieces, axis=0)
    return (stack, jnp.array(grown, dtype=jnp.int32))


def body(density, base_velocity, cells, offsets, target, stiffness, counts):
    size_x, size_y, size_z = density.shape
    capacity = cells.shape[1]
    anchor = jnp.stack(
        [lax.axis_index("gx") * size_x, lax.axis_index(GY) * size_y, lax.axis_index("gz") * size_z]
    )
    own_tables = make_tables(
        cells - anchor[:, None], offsets, 1, (size_x + 4, size_y + 4, size_z + 4)
    )
    live = (jnp.arange(capacity, dtype=jnp.int32) < counts[0]).astype(jnp.float32)
    scale = lax.rsqrt(density)
    stacked = jnp.concatenate([base_velocity, scale[None]], axis=0)
    fields = extended(stacked, (("gx", 1), (GY, 2), ("gz", 3)), 3)
    base_wide = fields[:3, 1 : size_x + 5, 1 : size_y + 5, 1 : size_z + 5]
    scale_wide = fields[3, 1 : size_x + 5, 1 : size_y + 5, 1 : size_z + 5]
    scale_full = fields[3]
    directions = moving_directions()
    block_sizes = jnp.array([size_x, size_y, size_z], dtype=jnp.int32)
    coordinates = (cells - anchor[:, None]).astype(jnp.float32)
    tables_all, tags = surround(jnp.concatenate([coordinates, offsets], axis=0))
    neighbour_local = (
        tables_all[:, :3].astype(jnp.int32) - (tags * block_sizes[None, :])[:, :, None]
    )
    neighbour_local = jnp.transpose(neighbour_local, (1, 0, 2)).reshape(3, -1)
    neighbour_fractions = jnp.transpose(tables_all[:, 3:], (1, 0, 2)).reshape(3, -1)
    neighbour_tables = make_tables(
        neighbour_local, neighbour_fractions, 2, (size_x + 6, size_y + 6, size_z + 6)
    )

    def spread_markers(vector):
        vectors_all, unused = surround(vector)
        flat_vectors = jnp.transpose(vectors_all, (1, 0, 2)).reshape(3, -1)
        return spread_dense(flat_vectors, neighbour_tables)

    def stream_wide(wide):
        post = jnp.zeros((3, size_x + 4, size_y + 4, size_z + 4), jnp.float32)
        for along_x, along_y, along_z, share in directions:
            piece = wide[
                :,
                1 - along_x : 5 - along_x + size_x,
                1 - along_y : 5 - along_y + size_y,
                1 - along_z : 5 - along_z + size_z,
            ]
            population = (
                3.0 * share * (along_x * piece[0] + along_y * piece[1] + along_z * piece[2])
            )
            post = post + jnp.stack(
                [along_x * population, along_y * population, along_z * population]
            )
        return scale_wide * (wide[:, 1 : size_x + 5, 1 : size_y + 5, 1 : size_z + 5] + post) * 0.5

    def apply(vector):
        wide = scale_full * spread_markers(vector)
        velocity_wide = stream_wide(wide)
        return live * (interpolate_dense(velocity_wide, own_tables) + stiffness * vector)

    def both_products(vector, image):
        return (
            one_axis_at_a_time(jnp.sum(vector * vector), GX_GY_GZ),
            one_axis_at_a_time(jnp.sum(vector * image), GX_GY_GZ),
        )

    right = live * (target - interpolate_dense(base_wide, own_tables))
    solution = jnp.zeros_like(right)
    residual = right
    image = apply(residual)
    norm_now, product = both_products(residual, image)
    alpha = norm_now / product
    direction = residual
    along = image
    for step in range(ITERS):
        solution = solution + alpha * direction
        residual = residual - alpha * along
        if step + 1 < ITERS:
            image = apply(residual)
            norm_next, product = both_products(residual, image)
            ratio = norm_next / norm_now
            alpha = norm_next / (product - ratio * norm_next / alpha)
            direction = residual + ratio * direction
            along = image + ratio * along
            norm_now = norm_next
    return solution


def solution(mesh):
    finer = Mesh(
        mesh.devices.reshape(mesh.shape["gx"], 4, 2, mesh.shape["gz"]), ("gx", "gy_0", "gy_1", "gz")
    )
    return jax.shard_map(
        body,
        mesh=finer,
        in_specs=(
            P("gx", GY, "gz"),
            P(None, "gx", GY, "gz"),
            P(None, GX_GY_GZ),
            P(None, GX_GY_GZ),
            P(None, GX_GY_GZ),
            P(GX_GY_GZ),
            P(GX_GY_GZ),
        ),
        out_specs=P(None, GX_GY_GZ),
        check_vma=False,
    )
```

profile of v0, /device:TPU:1, one launch (start us, length us, event | category | flops | bytes accessed | tf_op | source)
XLA Modules:
  0.0 326.5 jit_solution(7431941897793863222)
XLA Ops:
  0.1 0.8 fusion.530
  1.5 2.5 collective-permute-start.13
  4.0 4.0 %collective-permute-start.12 = (f32[1,6,256]{2,1,0:T(8,128)S(1)}, f32[1,6,256]{2,1,0:T(8,128)S(1)}, u32[]{:S(2)}, u32[]{:S(2)}) collective-permute-start(f32[1,6,256]{2,1,0:T(8,128)S(1)} %maximum_bitcast_fusion), channel_id=1, source_target_pairs={{0,224},{32,0},{64,32},{96,64},{128,96},{160,128},{192,160},{224,1... | collective-permute-start | bytes 18440 | tf_op jit(solution)/shard_map/ppermute | solution.py:14
  8.0 0.8 rsqrt_bitcast_fusion
  8.8 0.8 pad_maximum_fusion.7
  9.7 2.7 collective-permute-start.1
  12.3 0.9 subtract_multiply_fusion.12
  15.2 2.7 collective-permute-start.15
  17.9 3.2 collective-permute-done.14
  21.2 1.3 collective-permute-start.17
  22.4 1.6 collective-permute-start.16
  24.1 0.9 pad_maximum_fusion.2
  26.3 0.8 fusion.451
  29.1 34.5 %select_reduce_fusion = f32[6912,134]{0,1:T(8,128)S(1)} fusion(f32[4,6912]{1,0:T(4,128)S(1)} %pad_maximum_fusion.5, s32[4,6912]{1,0:T(4,128)S(1)} %add_add_fusion), kind=kLoop, calls=%fused_computation.6 | loop fusion | flops 10188288 | bytes 3926016 | tf_op jit(solution)/shard_map/reduce_sum | solution.py:70
  63.9 1.0 select_reduce_fusion.1
  65.2 1.2 collective-permute-start.4
  66.4 1.6 collective-permute-start.5
  68.0 1.0 select_reduce_fusion.2
  69.0 7.2 %collective-permute-done.4 = f32[4,14,14,3]{3,2,1,0:T(8,128)S(1)} collective-permute-done((f32[4,14,14,3]{3,2,1,0:T(8,128)S(1)}, f32[4,14,14,3]{3,2,1,0:T(8,128)S(1)}, u32[]{:S(2)}, u32[]{:S(2)}) %collective-permute-start.4) | collective-permute-done | bytes 9440 | tf_op jit(solution)/shard_map/ppermute | solution.py:24
  76.2 0.8 collective-permute-done.5
  78.4 2.7 collective-permute-start.6
  81.1 1.0 collective-permute-done.7
  82.1 5.1 %collective-permute-start.9 = (f32[3,3,256]{2,1,0:T(4,128)S(1)}, f32[3,3,256]{2,1,0:T(4,128)S(1)}, u32[]{:S(2)}, u32[]{:S(2)}) collective-permute-start(f32[3,3,256]{2,1,0:T(4,128)S(1)} %pad_maximum_fusion.9), channel_id=1, source_target_pairs={{0,4},{4,8},{8,12},{12,16},{16,20},{20,24},{24,28},{28,0},{1,5},{5... | collective-permute-start | bytes 27656 | tf_op jit(solution)/shard_map/ppermute | solution.py:14
  87.2 3.1 collective-permute-done.8
  90.3 2.5 collective-permute-start.10
  94.0 3.5 %collective-permute-done.11 = f32[9,3,256]{2,1,0:T(4,128)S(1)} collective-permute-done((f32[9,3,256]{2,1,0:T(4,128)S(1)}, f32[9,3,256]{2,1,0:T(4,128)S(1)}, u32[]{:S(2)}, u32[]{:S(2)}) %collective-permute-start.11) | collective-permute-done | bytes 27680 | tf_op jit(solution)/shard_map/ppermute | solution.py:14
  97.6 14.8 %fusion.15 = f32[3,14,14,134]{3,2,1,0:T(8,128)S(1)} fusion(f32[6912,134]{0,1:T(8,128)S(1)} %select_reduce_fusion, f32[14,6912]{1,0:T(8,128)S(1)} %bitcast.78, f32[3,14,6912]{2,1,0:T(8,128)S(1)} %broadcast_multiply_fusion.2, f32[14,14,134]{2,1,0:T(8,128)S(1)} %slice_bitcast_fusion), kind=kOutput, calls=%fused_computation.21 | convolution fusion | flops 6539466752 | bytes 5673344 | tf_op jit(solution)/shard_map/cxym,mz->cxyz/dot_general | solution.py:83
  113.1 1.0 broadcast_multiply_fusion.30
  115.4 0.8 broadcast_multiply_fusion.32
  116.6 1.7 fusion.31
  119.0 14.3 %all-reduce.2 = (f32[]{:T(128)}, f32[]{:T(128)}) all-reduce(f32[]{:T(128)} %get-tuple-element.13, f32[]{:T(128)} %get-tuple-element.12), channel_id=1, replica_groups=mesh['gx'=8,'gy_0'=4,'gy_1'=2,'gz'=4] {'gx'}, use_global_device_ids=true, to_apply=%region_5.0 | all-reduce | flops 2 | bytes 16 | tf_op jit(solution)/shard_map/psum | solution.py:35
  133.3 9.5 %all-reduce.8 = (f32[]{:T(128)}, f32[]{:T(128)}) all-reduce(f32[]{:T(128)} %get-tuple-element.18, f32[]{:T(128)} %get-tuple-element.19), channel_id=1, replica_groups=mesh['gx'=8,'gy_0'=4,'gy_1'=2,'gz'=4] {'gy_0'}, use_global_device_ids=true, to_apply=%region_6.0 | all-reduce | flops 2 | bytes 16 | tf_op jit(solution)/shard_map/psum | solution.py:35
  142.7 8.9 %all-reduce.11 = (f32[]{:T(128)}, f32[]{:T(128)}) all-reduce(f32[]{:T(128)} %get-tuple-element.30, f32[]{:T(128)} %get-tuple-element.31), channel_id=1, replica_groups=mesh['gx'=8,'gy_0'=4,'gy_1'=2,'gz'=4] {'gy_1'}, use_global_device_ids=true, to_apply=%region_7.0 | all-reduce | flops 2 | bytes 16 | tf_op jit(solution)/shard_map/psum | solution.py:35
  151.7 6.7 %all-reduce.5 = (f32[]{:T(128)}, f32[]{:T(128)}) all-reduce(f32[]{:T(128)} %get-tuple-element.36, f32[]{:T(128)} %get-tuple-element.37), channel_id=1, replica_groups=mesh['gx'=8,'gy_0'=4,'gy_1'=2,'gz'=4] {'gz'}, use_global_device_ids=true, to_apply=%region_8.0 | all-reduce | flops 2 | bytes 16 | tf_op jit(solution)/shard_map/psum | solution.py:35
  159.8 2.7 collective-permute-start.18
  162.5 1.0 collective-permute-done.19
  163.5 2.8 collective-permute-start.21
  166.7 2.7 collective-permute-done.20
  169.4 1.8 collective-permute-start.22
  171.5 1.0 collective-permute-done.22
  172.6 2.8 collective-permute-done.23
  175.6 17.1 %fusion.20 = f32[3,14,14,134]{3,2,1,0:T(8,128)S(1)} fusion(f32[6912,134]{0,1:T(8,128)} %copy-done, f32[3,14,6912]{2,1,0:T(8,128)S(1)} %broadcast_multiply_fusion.1, f32[14,6912]{1,0:T(8,128)S(1)} %bitcast.79, f32[14,14,134]{2,1,0:T(8,128)S(1)} %slice_bitcast_fusion), kind=kOutput, calls=%fused_computation.22 | convolution fusion | flops 6539466752 | bytes 5673344 | tf_op jit(solution)/shard_map/cxym,mz->cxyz/dot_general | solution.py:83
  193.3 1.0 broadcast_multiply_fusion.21
  195.6 0.8 broadcast_multiply_fusion.23
  196.8 1.7 fusion.32
  199.1 14.3 %all-reduce.1 = (f32[]{:T(128)}, f32[]{:T(128)}) all-reduce(f32[]{:T(128)} %get-tuple-element.11, f32[]{:T(128)} %get-tuple-element.10), channel_id=1, replica_groups=mesh['gx'=8,'gy_0'=4,'gy_1'=2,'gz'=4] {'gx'}, use_global_device_ids=true, to_apply=%region_19.0 | all-reduce | flops 2 | bytes 16 | tf_op jit(solution)/shard_map/psum | solution.py:35
  213.4 10.8 %all-reduce.7 = (f32[]{:T(128)}, f32[]{:T(128)}) all-reduce(f32[]{:T(128)} %get-tuple-element.16, f32[]{:T(128)} %get-tuple-element.17), channel_id=1, replica_groups=mesh['gx'=8,'gy_0'=4,'gy_1'=2,'gz'=4] {'gy_0'}, use_global_device_ids=true, to_apply=%region_20.0 | all-reduce | flops 2 | bytes 16 | tf_op jit(solution)/shard_map/psum | solution.py:35
  224.2 7.2 %all-reduce.10 = (f32[]{:T(128)}, f32[]{:T(128)}) all-reduce(f32[]{:T(128)} %get-tuple-element.28, f32[]{:T(128)} %get-tuple-element.29), channel_id=1, replica_groups=mesh['gx'=8,'gy_0'=4,'gy_1'=2,'gz'=4] {'gy_1'}, use_global_device_ids=true, to_apply=%region_21.0 | all-reduce | flops 2 | bytes 16 | tf_op jit(solution)/shard_map/psum | solution.py:35
  231.4 6.8 %all-reduce.4 = (f32[]{:T(128)}, f32[]{:T(128)}) all-reduce(f32[]{:T(128)} %get-tuple-element.34, f32[]{:T(128)} %get-tuple-element.35), channel_id=1, replica_groups=mesh['gx'=8,'gy_0'=4,'gy_1'=2,'gz'=4] {'gz'}, use_global_device_ids=true, to_apply=%region_22.0 | all-reduce | flops 2 | bytes 16 | tf_op jit(solution)/shard_map/psum | solution.py:35
  242.9 2.7 collective-permute-start.24
  245.5 1.0 collective-permute-done.25
  246.5 4.8 %collective-permute-start.27 = (f32[3,3,256]{2,1,0:T(4,128)S(1)}, f32[3,3,256]{2,1,0:T(4,128)S(1)}, u32[]{:S(2)}, u32[]{:S(2)}) collective-permute-start(f32[3,3,256]{2,1,0:T(4,128)S(1)} %pad_maximum_fusion.11), channel_id=1, source_target_pairs={{0,4},{4,8},{8,12},{12,16},{16,20},{20,24},{24,28},{28,0},{1,5},{5... | collective-permute-start | bytes 27656 | tf_op jit(solution)/shard_map/ppermute | solution.py:14
  251.3 3.1 collective-permute-done.26
  254.5 1.8 collective-permute-start.28
  256.5 1.4 collective-permute-done.28
  258.0 2.8 collective-permute-done.29
  260.9 16.9 %fusion.25 = f32[3,14,14,134]{3,2,1,0:T(8,128)S(1)} fusion(f32[6912,134]{0,1:T(8,128)} %copy-done, f32[3,14,6912]{2,1,0:T(8,128)S(1)} %broadcast_multiply_fusion, f32[14,6912]{1,0:T(8,128)S(1)} %bitcast.80, f32[14,14,134]{2,1,0:T(8,128)S(1)} %slice_bitcast_fusion), kind=kOutput, calls=%fused_computation.23 | convolution fusion | flops 6539466752 | bytes 5673344 | tf_op jit(solution)/shard_map/cxym,mz->cxyz/dot_general | solution.py:83
  278.5 1.0 broadcast_multiply_fusion.12
  280.8 0.8 broadcast_multiply_fusion.14
  281.9 1.7 fusion.33
  284.3 14.2 %all-reduce = (f32[]{:T(128)}, f32[]{:T(128)}) all-reduce(f32[]{:T(128)} %get-tuple-element.9, f32[]{:T(128)} %get-tuple-element.8), channel_id=1, replica_groups=mesh['gx'=8,'gy_0'=4,'gy_1'=2,'gz'=4] {'gx'}, use_global_device_ids=true, to_apply=%region_30.0 | all-reduce | flops 2 | bytes 16 | tf_op jit(solution)/shard_map/psum | solution.py:35
  298.5 8.6 %all-reduce.6 = (f32[]{:T(128)}, f32[]{:T(128)}) all-reduce(f32[]{:T(128)} %get-tuple-element.14, f32[]{:T(128)} %get-tuple-element.15), channel_id=1, replica_groups=mesh['gx'=8,'gy_0'=4,'gy_1'=2,'gz'=4] {'gy_0'}, use_global_device_ids=true, to_apply=%region_31.0 | all-reduce | flops 2 | bytes 16 | tf_op jit(solution)/shard_map/psum | solution.py:35
  307.2 7.8 %all-reduce.9 = (f32[]{:T(128)}, f32[]{:T(128)}) all-reduce(f32[]{:T(128)} %get-tuple-element.26, f32[]{:T(128)} %get-tuple-element.27), channel_id=1, replica_groups=mesh['gx'=8,'gy_0'=4,'gy_1'=2,'gz'=4] {'gy_1'}, use_global_device_ids=true, to_apply=%region_32.0 | all-reduce | flops 2 | bytes 16 | tf_op jit(solution)/shard_map/psum | solution.py:35
  314.9 6.7 %all-reduce.3 = (f32[]{:T(128)}, f32[]{:T(128)}) all-reduce(f32[]{:T(128)} %get-tuple-element.32, f32[]{:T(128)} %get-tuple-element.33), channel_id=1, replica_groups=mesh['gx'=8,'gy_0'=4,'gy_1'=2,'gz'=4] {'gz'}, use_global_device_ids=true, to_apply=%region_33.0 | all-reduce | flops 2 | bytes 16 | tf_op jit(solution)/shard_map/psum | solution.py:35
  (141 shorter events, 19.2 us)
Async XLA Ops:
  1.5 13.6 %collective-permute-start.13 = (f32[1,6,256]{2,1,0:T(8,128)S(1)}, f32[1,6,256]{2,1,0:T(8,128)S(1)}, u32[]{:S(2)}, u32[]{:S(2)}) collective-permute-start(f32[1,6,256]{2,1,0:T(8,128)S(1)} %maximum_bitcast_fusion), channel_id=1, source_target_pairs={{0,32},{32,64},{64,96},{96,128},{128,160},{160,192},{192,224},{224... | collective-permute-start | bytes 18440 | tf_op jit(solution)/shard_map/ppermute | solution.py:14
  4.0 11.2 %collective-permute-start.12 = (f32[1,6,256]{2,1,0:T(8,128)S(1)}, f32[1,6,256]{2,1,0:T(8,128)S(1)}, u32[]{:S(2)}, u32[]{:S(2)}) collective-permute-start(f32[1,6,256]{2,1,0:T(8,128)S(1)} %maximum_bitcast_fusion), channel_id=1, source_target_pairs={{0,224},{32,0},{64,32},{96,64},{128,96},{160,128},{192,160},{224,1... | collective-permute-start | bytes 18440 | tf_op jit(solution)/shard_map/ppermute | solution.py:14
  9.6 14.5 %collective-permute-start = (f32[4,3,8,128]{3,2,1,0:T(8,128)S(1)}, f32[4,3,8,128]{3,2,1,0:T(8,128)S(1)}, u32[]{:S(2)}, u32[]{:S(2)}) collective-permute-start(f32[4,3,8,128]{3,2,1,0:T(8,128)S(1)} %get-tuple-element.221), channel_id=1, source_target_pairs={{0,32},{32,64},{64,96},{96,128},{128,160},{160,192},{192,224},{224... | collective-permute-start | bytes 147464 | tf_op jit(solution)/shard_map/ppermute | solution.py:24
  9.7 14.4 %collective-permute-start.1 = (f32[4,3,8,128]{3,2,1,0:T(8,128)S(1)}, f32[4,3,8,128]{3,2,1,0:T(8,128)S(1)}, u32[]{:S(2)}, u32[]{:S(2)}) collective-permute-start(f32[4,3,8,128]{3,2,1,0:T(8,128)S(1)} %get-tuple-element.222), channel_id=1, source_target_pairs={{32,0},{64,32},{96,64},{128,96},{160,128},{192,160},{224,192},{0,2... | collective-permute-start | bytes 147464 | tf_op jit(solution)/shard_map/ppermute | solution.py:26
  15.2 6.0 %collective-permute-start.15 = (f32[3,6,256]{2,1,0:T(8,128)S(1)}, f32[3,6,256]{2,1,0:T(8,128)S(1)}, u32[]{:S(2)}, u32[]{:S(2)}) collective-permute-start(f32[3,6,256]{2,1,0:T(8,128)S(1)} %pad_maximum_fusion.8), channel_id=1, source_target_pairs={{0,4},{4,8},{8,12},{12,16},{16,20},{20,24},{24,28},{28,0},{1,5},{5... | collective-permute-start | bytes 55304 | tf_op jit(solution)/shard_map/ppermute | solution.py:14
  17.9 3.3 collective-permute-start.14
  21.2 5.1 %collective-permute-start.17 = (f32[9,6,256]{2,1,0:T(8,128)S(1)}, f32[9,6,256]{2,1,0:T(8,128)S(1)}, u32[]{:S(2)}, u32[]{:S(2)}) collective-permute-start(f32[9,6,256]{2,1,0:T(8,128)S(1)} %get-tuple-element.238), channel_id=1, source_target_pairs={{0,1},{1,2},{2,3},{3,0},{4,5},{5,6},{6,7},{7,4},{8,9},{9,10},{10,1... | collective-permute-start | bytes 165896 | tf_op jit(solution)/shard_map/ppermute | solution.py:14
  22.4 3.7 %collective-permute-start.16 = (f32[9,6,256]{2,1,0:T(8,128)S(1)}, f32[9,6,256]{2,1,0:T(8,128)S(1)}, u32[]{:S(2)}, u32[]{:S(2)}) collective-permute-start(f32[9,6,256]{2,1,0:T(8,128)S(1)} %get-tuple-element.238), channel_id=1, source_target_pairs={{0,3},{1,0},{2,1},{3,2},{4,7},{5,4},{6,5},{7,6},{8,11},{9,8},{10,9... | collective-permute-start | bytes 165896 | tf_op jit(solution)/shard_map/ppermute | solution.py:14
  25.0 39.9 %collective-permute-start.2 = (f32[4,14,3,128]{3,2,1,0:T(4,128)S(1)}, f32[4,14,3,128]{3,2,1,0:T(4,128)S(1)}, u32[]{:S(2)}, u32[]{:S(2)}) collective-permute-start(f32[4,14,3,128]{3,2,1,0:T(4,128)S(1)} %get-tuple-element.183), channel_id=1, source_target_pairs={{0,4},{4,8},{8,12},{12,16},{16,20},{20,24},{24,28},{28,0},{1,5},{5... | collective-permute-start | bytes 258056 | tf_op jit(solution)/shard_map/ppermute | solution.py:24
  25.6 39.3 %collective-permute-start.3 = (f32[4,14,3,128]{3,2,1,0:T(4,128)S(1)}, f32[4,14,3,128]{3,2,1,0:T(4,128)S(1)}, u32[]{:S(2)}, u32[]{:S(2)}) collective-permute-start(f32[4,14,3,128]{3,2,1,0:T(4,128)S(1)} %get-tuple-element.184), channel_id=1, source_target_pairs={{4,0},{8,4},{12,8},{16,12},{20,16},{24,20},{28,24},{0,28},{5,1},{9... | collective-permute-start | bytes 258056 | tf_op jit(solution)/shard_map/ppermute | solution.py:26
  26.1 38.8 %copy-start.1 = (f32[3,8,8,128]{3,2,1,0:T(8,128)S(1)}, f32[3,8,8,128]{3,2,1,0:T(8,128)}, u32[]{:S(2)}) copy-start(f32[3,8,8,128]{3,2,1,0:T(8,128)} %param.10) | copy-start | bytes 294916
  63.6 34.0 %copy-start = (f32[6912,134]{0,1:T(8,128)}, f32[6912,134]{0,1:T(8,128)S(1)}, u32[]{:S(2)}) copy-start(f32[6912,134]{0,1:T(8,128)S(1)} %select_reduce_fusion) | copy-start | bytes 11114500
  63.9 14.4 %copy-start.3 = (f32[3,256]{1,0:T(4,128)S(1)}, f32[3,256]{1,0:T(4,128)}, u32[]{:S(2)}) copy-start(f32[3,256]{1,0:T(4,128)} %param.13) | copy-start | bytes 9220
  65.2 11.0 %collective-permute-start.4 = (f32[4,14,14,3]{3,2,1,0:T(8,128)S(1)}, f32[4,14,14,3]{3,2,1,0:T(8,128)S(1)}, u32[]{:S(2)}, u32[]{:S(2)}) collective-permute-start(f32[4,14,14,3]{3,2,1,0:T(8,128)S(1)} %get-tuple-element.181), channel_id=1, source_target_pairs={{0,1},{1,2},{2,3},{3,0},{4,5},{5,6},{6,7},{7,4},{8,9},{9,10},{10,1... | collective-permute-start | bytes 28232 | tf_op jit(solution)/shard_map/ppermute | solution.py:24
  66.4 10.5 %collective-permute-start.5 = (f32[4,14,14,3]{3,2,1,0:T(8,128)S(1)}, f32[4,14,14,3]{3,2,1,0:T(8,128)S(1)}, u32[]{:S(2)}, u32[]{:S(2)}) collective-permute-start(f32[4,14,14,3]{3,2,1,0:T(8,128)S(1)} %get-tuple-element.182), channel_id=1, source_target_pairs={{1,0},{2,1},{3,2},{0,3},{5,4},{6,5},{7,6},{4,7},{9,8},{10,9},{11,1... | collective-permute-start | bytes 28232 | tf_op jit(solution)/shard_map/ppermute | solution.py:26
  78.3 3.7 %collective-permute-start.7 = (f32[1,3,256]{2,1,0:T(4,128)S(1)}, f32[1,3,256]{2,1,0:T(4,128)S(1)}, u32[]{:S(2)}, u32[]{:S(2)}) collective-permute-start(f32[1,3,256]{2,1,0:T(4,128)S(1)} %bitcast.81), channel_id=1, source_target_pairs={{0,32},{32,64},{64,96},{96,128},{128,160},{160,192},{192,224},{224... | collective-permute-start | bytes 9224 | tf_op jit(solution)/shard_map/ppermute | solution.py:14
  78.4 3.7 %collective-permute-start.6 = (f32[1,3,256]{2,1,0:T(4,128)S(1)}, f32[1,3,256]{2,1,0:T(4,128)S(1)}, u32[]{:S(2)}, u32[]{:S(2)}) collective-permute-start(f32[1,3,256]{2,1,0:T(4,128)S(1)} %bitcast.82), channel_id=1, source_target_pairs={{0,224},{32,0},{64,32},{96,64},{128,96},{160,128},{192,160},{224,1... | collective-permute-start | bytes 9224 | tf_op jit(solution)/shard_map/ppermute | solution.py:14
  82.1 8.2 %collective-permute-start.9 = (f32[3,3,256]{2,1,0:T(4,128)S(1)}, f32[3,3,256]{2,1,0:T(4,128)S(1)}, u32[]{:S(2)}, u32[]{:S(2)}) collective-permute-start(f32[3,3,256]{2,1,0:T(4,128)S(1)} %pad_maximum_fusion.9), channel_id=1, source_target_pairs={{0,4},{4,8},{8,12},{12,16},{16,20},{20,24},{24,28},{28,0},{1,5},{5... | collective-permute-start | bytes 27656 | tf_op jit(solution)/shard_map/ppermute | solution.py:14
  87.2 3.1 collective-permute-start.8
  90.3 3.6 %collective-permute-start.10 = (f32[9,3,256]{2,1,0:T(4,128)S(1)}, f32[9,3,256]{2,1,0:T(4,128)S(1)}, u32[]{:S(2)}, u32[]{:S(2)}) collective-permute-start(f32[9,3,256]{2,1,0:T(4,128)S(1)} %get-tuple-element.250), channel_id=1, source_target_pairs={{0,3},{1,0},{2,1},{3,2},{4,7},{5,4},{6,5},{7,6},{8,11},{9,8},{10,9... | collective-permute-start | bytes 82952 | tf_op jit(solution)/shard_map/ppermute | solution.py:14
  93.0 4.5 %collective-permute-start.11 = (f32[9,3,256]{2,1,0:T(4,128)S(1)}, f32[9,3,256]{2,1,0:T(4,128)S(1)}, u32[]{:S(2)}, u32[]{:S(2)}) collective-permute-start(f32[9,3,256]{2,1,0:T(4,128)S(1)} %get-tuple-element.250), channel_id=1, source_target_pairs={{0,1},{1,2},{2,3},{3,0},{4,5},{5,6},{6,7},{7,4},{8,9},{9,10},{10,1... | collective-permute-start | bytes 82952 | tf_op jit(solution)/shard_map/ppermute | solution.py:14
  116.6 1.7 copy-start.2
  159.8 3.7 %collective-permute-start.19 = (f32[1,3,256]{2,1,0:T(4,128)S(1)}, f32[1,3,256]{2,1,0:T(4,128)S(1)}, u32[]{:S(2)}, u32[]{:S(2)}) collective-permute-start(f32[1,3,256]{2,1,0:T(4,128)S(1)} %bitcast.84), channel_id=1, source_target_pairs={{0,32},{32,64},{64,96},{96,128},{128,160},{160,192},{192,224},{224... | collective-permute-start | bytes 9224 | tf_op jit(solution)/shard_map/ppermute | solution.py:14
  159.8 3.7 %collective-permute-start.18 = (f32[1,3,256]{2,1,0:T(4,128)S(1)}, f32[1,3,256]{2,1,0:T(4,128)S(1)}, u32[]{:S(2)}, u32[]{:S(2)}) collective-permute-start(f32[1,3,256]{2,1,0:T(4,128)S(1)} %bitcast.85), channel_id=1, source_target_pairs={{0,224},{32,0},{64,32},{96,64},{128,96},{160,128},{192,160},{224,1... | collective-permute-start | bytes 9224 | tf_op jit(solution)/shard_map/ppermute | solution.py:14
  163.5 5.9 %collective-permute-start.21 = (f32[3,3,256]{2,1,0:T(4,128)S(1)}, f32[3,3,256]{2,1,0:T(4,128)S(1)}, u32[]{:S(2)}, u32[]{:S(2)}) collective-permute-start(f32[3,3,256]{2,1,0:T(4,128)S(1)} %pad_maximum_fusion.10), channel_id=1, source_target_pairs={{0,4},{4,8},{8,12},{12,16},{16,20},{20,24},{24,28},{28,0},{1,5},{5... | collective-permute-start | bytes 27656 | tf_op jit(solution)/shard_map/ppermute | solution.py:14
  166.3 3.1 collective-permute-start.20
  169.4 3.2 collective-permute-start.22
  171.2 4.2 %collective-permute-start.23 = (f32[9,3,256]{2,1,0:T(4,128)S(1)}, f32[9,3,256]{2,1,0:T(4,128)S(1)}, u32[]{:S(2)}, u32[]{:S(2)}) collective-permute-start(f32[9,3,256]{2,1,0:T(4,128)S(1)} %get-tuple-element.246), channel_id=1, source_target_pairs={{0,1},{1,2},{2,3},{3,0},{4,5},{5,6},{6,7},{7,4},{8,9},{9,10},{10,1... | collective-permute-start | bytes 82952 | tf_op jit(solution)/shard_map/ppermute | solution.py:14
  242.8 3.7 %collective-permute-start.25 = (f32[1,3,256]{2,1,0:T(4,128)S(1)}, f32[1,3,256]{2,1,0:T(4,128)S(1)}, u32[]{:S(2)}, u32[]{:S(2)}) collective-permute-start(f32[1,3,256]{2,1,0:T(4,128)S(1)} %bitcast.93), channel_id=1, source_target_pairs={{0,32},{32,64},{64,96},{96,128},{128,160},{160,192},{192,224},{224... | collective-permute-start | bytes 9224 | tf_op jit(solution)/shard_map/ppermute | solution.py:14
  242.9 3.7 %collective-permute-start.24 = (f32[1,3,256]{2,1,0:T(4,128)S(1)}, f32[1,3,256]{2,1,0:T(4,128)S(1)}, u32[]{:S(2)}, u32[]{:S(2)}) collective-permute-start(f32[1,3,256]{2,1,0:T(4,128)S(1)} %bitcast.94), channel_id=1, source_target_pairs={{0,224},{32,0},{64,32},{96,64},{128,96},{160,128},{192,160},{224,1... | collective-permute-start | bytes 9224 | tf_op jit(solution)/shard_map/ppermute | solution.py:14
  246.5 7.9 %collective-permute-start.27 = (f32[3,3,256]{2,1,0:T(4,128)S(1)}, f32[3,3,256]{2,1,0:T(4,128)S(1)}, u32[]{:S(2)}, u32[]{:S(2)}) collective-permute-start(f32[3,3,256]{2,1,0:T(4,128)S(1)} %pad_maximum_fusion.11), channel_id=1, source_target_pairs={{0,4},{4,8},{8,12},{12,16},{16,20},{20,24},{24,28},{28,0},{1,5},{5... | collective-permute-start | bytes 27656 | tf_op jit(solution)/shard_map/ppermute | solution.py:14
  251.3 3.1 collective-permute-start.26
  254.5 3.5 %collective-permute-start.28 = (f32[9,3,256]{2,1,0:T(4,128)S(1)}, f32[9,3,256]{2,1,0:T(4,128)S(1)}, u32[]{:S(2)}, u32[]{:S(2)}) collective-permute-start(f32[9,3,256]{2,1,0:T(4,128)S(1)} %get-tuple-element.242), channel_id=1, source_target_pairs={{0,3},{1,0},{2,1},{3,2},{4,7},{5,4},{6,5},{7,6},{8,11},{9,8},{10,9... | collective-permute-start | bytes 82952 | tf_op jit(solution)/shard_map/ppermute | solution.py:14
  256.3 4.5 %collective-permute-start.29 = (f32[9,3,256]{2,1,0:T(4,128)S(1)}, f32[9,3,256]{2,1,0:T(4,128)S(1)}, u32[]{:S(2)}, u32[]{:S(2)}) collective-permute-start(f32[9,3,256]{2,1,0:T(4,128)S(1)} %get-tuple-element.242), channel_id=1, source_target_pairs={{0,1},{1,2},{2,3},{3,0},{4,5},{5,6},{6,7},{7,4},{8,9},{9,10},{10,1... | collective-permute-start | bytes 82952 | tf_op jit(solution)/shard_map/ppermute | solution.py:14
where the time goes:
time: 333 us; the launch traced here: 326 us
  blocking collectives  116 us (35%)
  other arithmetic  60.4 us (18%)
  matrix products  54.6 us (16%)
  starting transfers between devices  46.7 us (14%)
  waiting for transfers between devices  35.7 us (11%)
  between operations  11.6 us (3%)
    psum x12, blocking collectives, one_axis_at_a_time(): shard = lax.psum(shard, axis)  116 us
    dot_general x3, matrix products, spread_dense(): jnp.einsum('cxym,mz->cxyz', weighted, table_z, precision=lax.Precision.HI...  48.7 us
    ppermute x24, starting transfers between devices, shifted(): lax.ppermute(shard, axis, [(i, (i + by) % length) for i in range(length)])  40.6 us
    reduce_sum x6, other arithmetic, axis_rows(): return jnp.sum(delta_weights(fraction)[:, :, None] * hits, axis=0)  37 us
    ppermute x24, waiting for transfers between devices, shifted(): lax.ppermute(shard, axis, [(i, (i + by) % length) for i in range(length)])  27.7 us
    mul x15, other arithmetic, stream_wide(): 3.0 * share * (along_x * piece[0] + along_y * piece[1] + along_z * piece[2])  7.43 us
    ppermute x3, waiting for transfers between devices, extended(): lax.ppermute(tail, axis, [(i, (i + 1) % count) for i in range(count)])  7.18 us
  transfers between devices with their start and end apart: 30, of which 17 were waited for; matrix products, arithmetic and copies ran while one was open for 14% of the time, Pallas kernels for 0%

commit v1 on v0

v1 whole, which is shorter than its diff:
```python
import functools

import jax
import jax.numpy as jnp
from jax import lax
from jax.experimental import pallas as pl
from jax.experimental.pallas import tpu as pltpu
from jax.sharding import PartitionSpec as P

ITERS = 3
CX, CY, CZ = 8, 8, 128
CAP = 256
WX, WY, WZ = 13, 16, 256
TZ = 144
AXES = ("gx", "gy", "gz")
ALL = ("gx", "gy", "gz")
MESH = pl.DeviceIdType.MESH
SHIFT = 0.1
F32, BF16 = jnp.float32, jnp.bfloat16

GROUPS = [(dx, dy) for dx in (-1, 0, 1) for dy in (-1, 0, 1)]
DZS = (-1, 1, 0)
ORDER = sorted(range(9), key=lambda g: abs(GROUPS[g][0]) + abs(GROUPS[g][1]))
PLANES = {-1: (0, 4), 0: (1, 12), 1: (9, 4)}
ROWS = {-1: (0, 8), 0: (0, 16), 1: (8, 8)}
TAKE = {-1: (6, 8), 0: (0, 8), 1: (0, 3)}


def group_of(dx, dy):
    return (dx + 1) * 3 + dy + 1


def slot_of(dx, dy, dz):
    return group_of(dx, dy) * 3 + DZS.index(dz)


NEIGHBOURS = [
    (GROUPS[g][0], GROUPS[g][1], dz)
    for g in ORDER
    for dz in DZS
    if (GROUPS[g][0], GROUPS[g][1], dz) != (0, 0, 0)
]
CENTRE = group_of(0, 0)
SPANS = [PLANES[dx][1] * ROWS[dy][1] for dx, dy in GROUPS]
STARTS = [sum(SPANS[:g]) for g in range(9)]


def split(value):
    high = value.astype(BF16)
    return high, (value - high.astype(F32)).astype(BF16)


def dot3(lh, ll, rh, rl, dims):
    dot = functools.partial(
        lax.dot_general, dimension_numbers=(dims, ((), ())), preferred_element_type=F32
    )
    return dot(lh, rh) + (dot(ll, rh) + dot(lh, rl))


def kernel(
    sizes,
    density_ref, base_ref, cells_ref, offsets_ref, target_ref, stiff_ref, counts_ref,
    out_ref,
    field, ftrans, pack_z, mark_own, recv_f, recv_z, marks, main, halo, ztile, wide,
    table_h, table_l, own_h, own_l, wxy, left_h, left_l, grid, moved, plane_a, plane_b, plane_c,
    vel_h, vel_l, vecs, images, recv_v, part, recv_a, part_b, recv_b,
    send_f, got_f, send_z, got_z, send_m, got_m, send_v, got_v, send_r, got_r,
):
    size_x, size_y, size_z = sizes
    ix, iy, iz = (lax.axis_index(a) for a in AXES)

    def at(dx, dy, dz):
        return (
            lax.rem(ix + dx + size_x, size_x),
            lax.rem(iy + dy + size_y, size_y),
            lax.rem(iz + dz + size_z, size_z),
        )

    def mate(k):
        rest = lax.rem(iy * size_z + iz + k, size_y * size_z)
        return (ix, rest // size_z, lax.rem(rest, size_z))

    def along(k):
        return (lax.rem(ix + k, size_x), iy, iz)

    barrier = pltpu.get_barrier_semaphore()
    for offset in NEIGHBOURS:
        pl.semaphore_signal(barrier, inc=1, device_id=at(*offset), device_id_type=MESH)

    def greet_mate(k, carry):
        pl.semaphore_signal(barrier, inc=1, device_id=mate(k), device_id_type=MESH)
        return carry

    lax.fori_loop(1, size_y * size_z, greet_mate, 0)
    for k in range(1, size_x):
        pl.semaphore_signal(barrier, inc=1, device_id=along(k), device_id_type=MESH)

    field[0:3] = base_ref[...]
    field[3] = lax.rsqrt(density_ref[...])
    ftrans[...] = field[...].reshape(4 * CX * CY, CZ).T
    pack_z[0:2] = ftrans[CZ - 2 : CZ]
    pack_z[2:8] = ftrans[0:6]
    anchors = (ix * CX, iy * CY, iz * CZ)
    for k in range(3):
        mark_own[k : k + 1] = (cells_ref[k : k + 1] - anchors[k]).astype(F32)
    mark_own[3:6] = offsets_ref[...]
    mark_own[6:8] = jnp.zeros((2, CAP), F32)
    marks[slot_of(0, 0, 0)] = mark_own[...]

    pl.semaphore_wait(barrier, len(NEIGHBOURS) + size_y * size_z - 1 + size_x - 1)

    def remote(src, dst, send, recv, device):
        return pltpu.make_async_remote_copy(
            src_ref=src, dst_ref=dst, send_sem=send, recv_sem=recv, device_id=device,
            device_id_type=MESH,
        )

    def drain(ref, sem):
        pltpu.make_async_copy(ref, ref, sem).wait()

    def halo_copy(dx, dy):
        a, b = TAKE[-dx]
        g = group_of(-dx, -dy)
        return remote(
            field.at[:, a:b], recv_f.at[g, :, a:b], send_f.at[g], got_f.at[g], at(dx, dy, 0)
        )

    for dx, dy in GROUPS:
        if (dx, dy) != (0, 0):
            halo_copy(dx, dy).start()
    for dx, dy, dz in NEIGHBOURS:
        back = slot_of(-dx, -dy, -dz)
        if dz:
            remote(
                pack_z, recv_z.at[group_of(-dx, -dy) * 2 + DZS.index(-dz)], send_z, got_z, at(dx, dy, dz)
            ).start()
        remote(mark_own, marks.at[back], send_m, got_m, at(dx, dy, dz)).start()

    table_h[...] = jnp.zeros(table_h.shape, BF16)
    table_l[...] = jnp.zeros(table_l.shape, BF16)
    own_h[...] = jnp.zeros(own_h.shape, BF16)
    own_l[...] = jnp.zeros(own_l.shape, BF16)
    ztile[...] = jnp.zeros(ztile.shape, F32)
    main[:, :, 8:16] = jnp.zeros((4, WX, 8, CZ), F32)
    halo[:, :, 8:16] = jnp.zeros((4, WX, 8, CZ), F32)
    grid[...] = jnp.zeros(grid.shape, F32)
    vecs[...] = jnp.zeros(vecs.shape, F32)

    live = (lax.broadcasted_iota(jnp.int32, (1, CAP), 1) < counts_ref[0]).astype(F32)
    stiff = stiff_ref[...]

    def axis_table(first, rows, start, weights):
        away = (
            lax.broadcasted_iota(jnp.int32, (rows, CAP), 0).astype(F32) + float(first) - start
        )
        value = jnp.zeros((rows, CAP), F32)
        for step in range(4):
            value = jnp.where(away == float(step), weights[step], value)
        return value

    def build(g, j):
        (dx, dy), dz = GROUPS[g], DZS[j]
        mark = marks[g * 3 + j]
        fraction = mark[3:6]
        root = jnp.sqrt(1.0 + 4.0 * fraction - 4.0 * fraction * fraction)
        weights = [
            (3.0 - 2.0 * fraction - root) * 0.125,
            (3.0 - 2.0 * fraction + root) * 0.125,
            (1.0 + 2.0 * fraction + root) * 0.125,
            (1.0 + 2.0 * fraction - root) * 0.125,
        ]
        of = lambda k: [w[k : k + 1] for w in weights]
        x0, nx = PLANES[dx]
        y0, ny = ROWS[dy]
        table_x = axis_table(x0, 16, mark[0:1] + float(1 + CX * dx), of(0))
        table_y = axis_table(y0, ny, mark[1:2] + float(1 + CY * dy), of(1))
        lanes = slice(j * CAP, (j + 1) * CAP)
        for x in range(nx):
            at_row = STARTS[g] + x * ny
            wxy[at_row : at_row + ny, lanes] = table_x[x : x + 1] * table_y
        z0, nz = {-1: (0, 16), 0: (0, TZ), 1: (CZ, 16)}[dz]
        high, low = split(axis_table(z0, nz, mark[2:3] + float(1 + CZ * dz), of(2)))
        table_h[g, z0 : z0 + nz, lanes] = high
        table_l[g, z0 : z0 + nz, lanes] = low
        if g == CENTRE and dz == 0:
            own_h[0:TZ] = high
            own_l[0:TZ] = low

    build(CENTRE, 2)

    for g, (dx, dy) in enumerate(GROUPS):
        if g != CENTRE:
            halo_copy(-dx, -dy).wait_recv()
    drain(recv_z, got_z)
    low_rows = lax.broadcasted_iota(jnp.int32, (8, 4 * CX * CY), 0) < 2
    for g, (dx, dy) in enumerate(GROUPS):
        (xa, xb), (ya, yb) = TAKE[dx], TAKE[dy]
        x0, y0 = xa + CX * dx + 2, ya + CY * dy + 2
        source = field if g == CENTRE else recv_f.at[g]
        main[:, x0 : x0 + xb - xa, y0 : y0 + yb - ya] = source[:, xa:xb, ya:yb]
        columns = jnp.where(low_rows, recv_z[2 * g], recv_z[2 * g + 1])
        ztile[:, :, :, 0:8] = columns.T.reshape(4, CX, CY, 8)
        halo[:, x0 : x0 + xb - xa, y0 : y0 + yb - ya] = ztile[:, xa:xb, ya:yb]
    lane = lax.broadcasted_iota(jnp.int32, (WY, CZ), 1)

    def widen(x, carry):
        for c in range(4):
            turned = pltpu.roll(main[c, x], 2, 1)
            edge = halo[c, x]
            wide[c, x, :, 0:CZ] = jnp.where(lane < 2, edge, turned)
            wide[c, x, :, CZ:] = jnp.where(lane < 2, turned, jnp.where(lane < 5, edge, 0.0))
        return carry

    lax.fori_loop(0, WX, widen, 0)

    def interpolate():
        high = vel_h[...].reshape(3 * 11 * WY, WZ)
        low = vel_l[...].reshape(3 * 11 * WY, WZ)
        rows = dot3(high, low, own_h[...], own_l[...], ((1,), (0,)))
        weight = wxy[STARTS[CENTRE] : STARTS[CENTRE] + 11 * WY, 2 * CAP : 3 * CAP]
        return [
            jnp.sum(rows[c * 11 * WY : (c + 1) * 11 * WY] * weight, axis=0, keepdims=True)
            for c in range(3)
        ]

    for c in range(3):
        high, low = split(wide[c, 1:12])
        vel_h[c] = high
        vel_l[c] = low
    for c, value in enumerate(interpolate()):
        vecs[0, c : c + 1] = live * (target_ref[c : c + 1] - value)

    drain(marks.at[0:26], got_m)

    def send_vector(a):
        for dx, dy, dz in NEIGHBOURS:
            back = slot_of(-dx, -dy, -dz)
            remote(
                vecs.at[a], recv_v.at[a, back], send_v.at[a], got_v.at[a, back // 3], at(dx, dy, dz)
            ).start()
        recv_v[a, slot_of(0, 0, 0)] = vecs[a]

    def spread(a):
        grid[:, :, :, 0:TZ] = jnp.zeros((3, WX, WY, TZ), F32)
        for g in ORDER:
            (dx, dy) = GROUPS[g]
            if g == CENTRE:
                drain(recv_v.at[a, 3 * g : 3 * g + 2], got_v.at[a, g])
            else:
                drain(recv_v.at[a, 3 * g : 3 * g + 3], got_v.at[a, g])
            span = SPANS[g]
            for j in range(3):
                lanes = slice(j * CAP, (j + 1) * CAP)
                vector = recv_v[a, 3 * g + j]
                weight = wxy[STARTS[g] : STARTS[g] + span, lanes]
                for c in range(3):
                    high, low = split(weight * vector[c : c + 1])
                    left_h[c * span : (c + 1) * span, lanes] = high
                    left_l[c * span : (c + 1) * span, lanes] = low
            total = dot3(
                left_h[0 : 3 * span], left_l[0 : 3 * span], table_h[g], table_l[g], ((1,), (1,))
            )
            x0, nx = PLANES[dx]
            y0, ny = ROWS[dy]
            for c in range(3):
                at_place = (c, slice(x0, x0 + nx), slice(y0, y0 + ny), slice(0, TZ))
                grid[at_place] += total[c * span : (c + 1) * span].reshape(nx, ny, TZ)

    def shifts(value, axis):
        length = value.shape[axis]
        return pltpu.roll(value, 1, axis), pltpu.roll(value, length - 1, axis)

    def both(value, axis):
        before, after = shifts(value, axis)
        return before + after

    def stream():
        def planes(x, carry):
            scale = wide[3, x]
            m0, m1, m2 = (scale * grid[c, x] for c in range(3))
            moved[0, x], moved[1, x], moved[2, x] = m0, m1, m2
            before, after = shifts(m0, 0)
            sy0, dy0 = before + after, before - after
            before, after = shifts(m1, 0)
            sy1, dy1 = before + after, before - after
            before, after = shifts(m0, 1)
            sz0, dz0 = before + after, before - after
            before, after = shifts(m2, 1)
            sz2, dz2 = before + after, before - after
            before, after = shifts(dz2, 0)
            dyz2 = before - after
            before, after = shifts(dy1, 1)
            dyz1 = before - after
            plane_a[0, x] = 2.0 * m0 + sy0 + sz0
            plane_b[0, x] = dy1 + dz2
            plane_a[1, x] = sy1
            plane_b[1, x] = dy0
            plane_c[0, x] = 2.0 * sy1 + both(sy1, 1) + dyz2
            plane_a[2, x] = sz2
            plane_b[2, x] = dz0
            plane_c[1, x] = 2.0 * sz2 + both(sz2, 0) + dyz1
            return carry

        lax.fori_loop(0, WX, planes, 0)

        def velocity(x, carry):
            half = wide[3, x] * 0.5
            for c in range(3):
                post = plane_a[c, x - 1] + plane_a[c, x + 1] + plane_b[c, x - 1] - plane_b[c, x + 1]
                if c:
                    post = post + plane_c[c - 1, x]
                high, low = split(half * (moved[c, x] + post * (1.0 / 12.0)))
                vel_h[c, x - 1] = high
                vel_l[c, x - 1] = low
            return carry

        lax.fori_loop(1, 12, velocity, 0)

    def apply(a, carry):
        send_vector(a)

        @pl.when(a == 0)
        def _():
            for g in ORDER:
                for j in range(3):
                    if (g, j) != (CENTRE, 2):
                        build(g, j)

        spread(a)
        stream()
        for c, value in enumerate(interpolate()):
            vector = vecs[a, c : c + 1]
            image = live * (value + stiff * vector)
            images[a, c : c + 1] = image
            vecs[a + 1, c : c + 1] = image - SHIFT * vector
        return carry

    lax.fori_loop(0, ITERS, apply, 0)

    lane_row = lax.broadcasted_iota(jnp.int32, (1, 128), 1)
    v = [vecs[k, 0:3] for k in range(3)]
    w = [images[k, 0:3] for k in range(3)]
    pairs = [(v[i], w[j]) for i in range(3) for j in range(i, 3)] + [(v[0], v[j]) for j in range(3)]
    row = jnp.zeros((1, 128), F32)
    for k, (left, right) in enumerate(pairs):
        row = jnp.where(lane_row == k, jnp.sum(left * right), row)
    me = iy * size_z + iz
    part[...] = row
    recv_a[me] = row

    def send_mate(k, carry):
        remote(part, recv_a.at[me], send_r.at[0], got_r.at[0], mate(k)).start()
        return carry

    lax.fori_loop(1, size_y * size_z, send_mate, 0)
    drain(recv_a.at[0 : size_y * size_z - 1], got_r.at[0])
    total = jnp.sum(recv_a[...], axis=0)
    part_b[...] = total
    recv_b[ix] = total
    for k in range(1, size_x):
        remote(part_b, recv_b.at[ix], send_r.at[1], got_r.at[1], along(k)).start()
    drain(recv_b.at[0 : size_x - 1], got_r.at[1])
    total = jnp.sum(recv_b[...], axis=0)
    h00, h01, h02, h11, h12, h22, b0, b1, b2 = (
        jnp.sum(jnp.where(lane_row == k, total, 0.0), axis=1, keepdims=True) for k in range(9)
    )

    def over(top, pivot, size):
        fine = pivot > 1e-7 * size
        return jnp.where(fine, top / jnp.where(fine, pivot, 1.0), 0.0)

    l10 = over(h01, h00, h00)
    l20 = over(h02, h00, h00)
    d1 = h11 - l10 * h01
    e12 = h12 - l10 * h02
    l21 = over(e12, d1, h11)
    d2 = h22 - l20 * h02 - l21 * e12
    z1 = b1 - l10 * b0
    z2 = b2 - l20 * b0 - l21 * z1
    y2 = over(z2, d2, h22)
    y1 = over(z1, d1, h11) - l21 * y2
    y0 = over(b0, h00, h00) - l10 * y1 - l20 * y2
    out_ref[...] = y0 * v[0] + y1 * v[1] + y2 * v[2]

    for dx, dy in GROUPS:
        if (dx, dy) != (0, 0):
            halo_copy(dx, dy).wait_send()
    drain(recv_z, send_z)
    drain(marks.at[0:26], send_m)
    for a in range(ITERS):
        drain(recv_v.at[a, 0:26], send_v.at[a])
    drain(recv_a.at[0 : size_y * size_z - 1], send_r.at[0])
    drain(recv_b.at[0 : size_x - 1], send_r.at[1])


def solution(mesh):
    sizes = tuple(mesh.shape[a] for a in AXES)
    plane = sizes[1] * sizes[2]

    def body(density, base_velocity, cells, offsets, target, stiffness, counts):
        vmem = pl.BlockSpec(memory_space=pltpu.VMEM)
        return pl.pallas_call(
            functools.partial(kernel, sizes),
            out_shape=jax.ShapeDtypeStruct((3, CAP), F32),
            in_specs=[vmem] * 6 + [pl.BlockSpec(memory_space=pltpu.SMEM)],
            out_specs=vmem,
            scratch_shapes=[
                pltpu.VMEM((4, CX, CY, CZ), F32),
                pltpu.VMEM((CZ, 4 * CX * CY), F32),
                pltpu.VMEM((8, 4 * CX * CY), F32),
                pltpu.VMEM((8, CAP), F32),
                pltpu.VMEM((9, 4, CX, CY, CZ), F32),
                pltpu.VMEM((18, 8, 4 * CX * CY), F32),
                pltpu.VMEM((27, 8, CAP), F32),
                pltpu.VMEM((4, WX, WY, CZ), F32),
                pltpu.VMEM((4, WX, WY, CZ), F32),
                pltpu.VMEM((4, CX, CY, CZ), F32),
                pltpu.VMEM((4, WX, WY, WZ), F32),
                pltpu.VMEM((9, TZ, 3 * CAP), BF16),
                pltpu.VMEM((9, TZ, 3 * CAP), BF16),
                pltpu.VMEM((WZ, CAP), BF16),
                pltpu.VMEM((WZ, CAP), BF16),
                pltpu.VMEM((sum(SPANS), 3 * CAP), F32),
                pltpu.VMEM((3 * max(SPANS), 3 * CAP), BF16),
                pltpu.VMEM((3 * max(SPANS), 3 * CAP), BF16),
                pltpu.VMEM((3, WX, WY, WZ), F32),
                pltpu.VMEM((3, WX, WY, WZ), F32),
                pltpu.VMEM((3, WX, WY, WZ), F32),
                pltpu.VMEM((3, WX, WY, WZ), F32),
                pltpu.VMEM((2, WX, WY, WZ), F32),
                pltpu.VMEM((3, 11, WY, WZ), BF16),
                pltpu.VMEM((3, 11, WY, WZ), BF16),
                pltpu.VMEM((ITERS + 1, 4, CAP), F32),
                pltpu.VMEM((ITERS, 4, CAP), F32),
                pltpu.VMEM((ITERS, 27, 4, CAP), F32),
                pltpu.VMEM((1, 128), F32),
                pltpu.VMEM((plane, 1, 128), F32),
                pltpu.VMEM((1, 128), F32),
                pltpu.VMEM((sizes[0], 1, 128), F32),
                pltpu.SemaphoreType.DMA((9,)),
                pltpu.SemaphoreType.DMA((9,)),
                pltpu.SemaphoreType.DMA,
                pltpu.SemaphoreType.DMA,
                pltpu.SemaphoreType.DMA,
                pltpu.SemaphoreType.DMA,
                pltpu.SemaphoreType.DMA((ITERS,)),
                pltpu.SemaphoreType.DMA((ITERS, 9)),
                pltpu.SemaphoreType.DMA((2,)),
                pltpu.SemaphoreType.DMA((2,)),
            ],
            compiler_params=pltpu.CompilerParams(
                collective_id=0, has_side_effects=True, vmem_limit_bytes=60 * 1024 * 1024
            ),
            name="immersed",
        )(density, base_velocity, cells, offsets, target, stiffness[None], counts)

    return jax.shard_map(
        body,
        mesh=mesh,
        in_specs=(
            P(*AXES), P(None, *AXES), P(None, ALL), P(None, ALL), P(None, ALL), P(ALL), P(ALL),
        ),
        out_specs=P(None, ALL),
        check_vma=False,
    )
```

time: 333 us -> 69.4 us (0.21); the launches traced: 326 us -> 69.2 us
  blocking collectives: 116 us -> 0 us
  Pallas kernels: 0 us -> 67.3 us
  other arithmetic: 60.4 us -> 0 us
  matrix products: 54.6 us -> 0 us
  starting transfers between devices: 46.7 us -> 0 us
  waiting for transfers between devices: 35.7 us -> 0 us
  between operations: 11.6 us -> 0.66 us
    psum x12 -> x0, blocking collectives: 116 us -> none  [one_axis_at_a_time(): shard = lax.psum(shard, axis)]
    pallas_call x0 -> x1, Pallas kernels: none -> 67.3 us  [body(): pl.pallas_call(functools.partial(kernel, sizes), out_shape=jax.ShapeDtype...]
    dot_general x7 -> x0, matrix products: 54.6 us -> none  [the longest x3 48.7 us: spread_dense(): jnp.einsum('cxym,mz->cxyz', weighted, table_z, precision=lax.Precision.HI...]
    ppermute x30 -> x0, starting transfers between devices: 46.7 us -> none  [the longest x24 40.6 us: shifted(): lax.ppermute(shard, axis, [(i, (i + by) % length) for i in range(length)])]
    reduce_sum x9 -> x0, other arithmetic: 39 us -> none  [the longest x6 37 us: axis_rows(): return jnp.sum(delta_weights(fraction)[:, :, None] * hits, axis=0)]
    ppermute x30 -> x0, waiting for transfers between devices: 35.7 us -> none  [the longest x24 27.7 us: shifted(): lax.ppermute(shard, axis, [(i, (i + by) % length) for i in range(length)])]
    mul x37 -> x0, other arithmetic: 12.5 us -> none  [the longest x15 7.43 us: stream_wide(): 3.0 * share * (along_x * piece[0] + along_y * piece[1] + along_z * piece[2])]
  transfers between devices with their start and end apart: 30 -> 0, of which waited for: 17 -> 0; matrix products, arithmetic and copies ran while one was open for 14% -> 0% of each run, Pallas kernels for 0% -> 0%
where the time goes in v1:
time: 69.4 us; the launch traced here: 69.2 us
  Pallas kernels  67.3 us (97%)
  local copies, waits for them, and re-layouts  1.28 us (2%)
    pallas_call x1, Pallas kernels, body(): pl.pallas_call(functools.partial(kernel, sizes), out_shape=jax.ShapeDtype...  67.3 us

profile of v1, /device:TPU:1, one launch (start us, length us, event | category | flops | bytes accessed | tf_op | source)
XLA Modules:
  0.0 69.2 jit_solution(17701054115038451100)
XLA Ops:
  0.7 67.3 %immersed.1 = f32[3,256]{1,0:T(4,128)} custom-call(f32[8,8,128]{2,1,0:T(8,128)} %density_ref.1, f32[3,8,8,128]{3,2,1,0:T(8,128)} %base_ref.1, s32[3,256]{1,0:T(4,128)} %cells_ref.1, f32[3,256]{1,0:T(4,128)} %offsets_ref.1, f32[3,256]{1,0:T(4,128)} %target_ref.1, f32[1,256]{1,0:T(1,128)} %bitcast.1, s32[1]{0:T(128)S(6)} %copy.9.counts_ref), custom_call_target="tpu_custom_call" | custom-call | tf_op jit(solution)/shard_map/immersed/pallas_call | solution.py:402
  67.9 1.3 %copy.10 = f32[3,256]{1,0:T(4,128)} copy(f32[3,256]{1,0:T(4,128)} %immersed.1) | data formatting | bytes 6144

commit v2 on v1

--- a/solution.py
+++ b/solution.py
@@ -59,12 +59,14 @@
 
 def kernel(
     sizes,
-    density_ref, base_ref, cells_ref, offsets_ref, target_ref, stiff_ref, counts_ref,
+    density_in, base_in, cells_in, offsets_in, target_in, stiff_in, counts_ref,
     out_ref,
-    field, ftrans, pack_z, mark_own, recv_f, recv_z, marks, main, halo, ztile, wide,
-    table_h, table_l, own_h, own_l, wxy, left_h, left_l, grid, moved, plane_a, plane_b, plane_c,
-    vel_h, vel_l, vecs, images, recv_v, part, recv_a, part_b, recv_b,
-    send_f, got_f, send_z, got_z, send_m, got_m, send_v, got_v, send_r, got_r,
+    density_ref, cells_ref, offsets_ref, target_ref, stiff_ref,
+    field, ftrans, pack_lo, pack_hi, pack_z_lo, pack_z_hi, mark_own, recv_x, recv_lo, recv_hi,
+    recv_z_lo, recv_z_hi, columns, marks, main, halo, ztile, wide,
+    table_h, table_l, own_h, own_l, wxy, wxy_h, wxy_l, edge_w, left_h, left_l, grid, edges, moved, plane_a, plane_b, plane_c,
+    vel_h, vel_l, energy_ref, vecs, images, recv_v, part, recv_a, part_b, recv_b,
+    loaded, send_f, got_f, send_z, got_z, send_m, got_m, send_v, got_v, send_r, got_r,
 ):
     size_x, size_y, size_z = sizes
     ix, iy, iz = (lax.axis_index(a) for a in AXES)
@@ -83,6 +85,21 @@
     def along(k):
         return (lax.rem(ix + k, size_x), iy, iz)
 
+    loads = [
+        pltpu.make_async_copy(base_in.at[c], field.at[:, c], loaded.at[c]) for c in range(3)
+    ]
+    loads += [
+        pltpu.make_async_copy(source, target, loaded.at[3 + k])
+        for k, (source, target) in enumerate(
+            [
+                (density_in, density_ref), (cells_in, cells_ref), (offsets_in, offsets_ref),
+                (target_in, target_ref), (stiff_in, stiff_ref),
+            ]
+        )
+    ]
+    for load in loads:
+        load.start()
+
     barrier = pltpu.get_barrier_semaphore()
     for offset in NEIGHBOURS:
         pl.semaphore_signal(barrier, inc=1, device_id=at(*offset), device_id_type=MESH)
@@ -95,11 +112,15 @@
     for k in range(1, size_x):
         pl.semaphore_signal(barrier, inc=1, device_id=along(k), device_id_type=MESH)
 
-    field[0:3] = base_ref[...]
-    field[3] = lax.rsqrt(density_ref[...])
+    for load in loads:
+        load.wait()
+    field[:, 3] = lax.rsqrt(density_ref[...])
     ftrans[...] = field[...].reshape(4 * CX * CY, CZ).T
-    pack_z[0:2] = ftrans[CZ - 2 : CZ]
-    pack_z[2:8] = ftrans[0:6]
+    pack_z_lo[...] = ftrans[CZ - 2 : CZ]
+    pack_z_hi[...] = ftrans[0:4]
+    for c in range(4):
+        pack_lo[:, 2 * c : 2 * c + 2] = field[:, c, CY - 2 : CY]
+        pack_hi[:, 4 * c : 4 * c + 4] = field[:, c, 0:4]
     anchors = (ix * CX, iy * CY, iz * CZ)
     for k in range(3):
         mark_own[k : k + 1] = (cells_ref[k : k + 1] - anchors[k]).astype(F32)
@@ -121,29 +142,42 @@
     def halo_copy(dx, dy):
         a, b = TAKE[-dx]
         g = group_of(-dx, -dy)
-        return remote(
-            field.at[:, a:b], recv_f.at[g, :, a:b], send_f.at[g], got_f.at[g], at(dx, dy, 0)
-        )
+        if dy == 0:
+            pair = field.at[a:b], recv_x.at[dx == -1 and 1 or 0, a:b]
+        elif dy == 1:
+            pair = pack_lo.at[a:b], recv_lo.at[1 - dx, a:b]
+        else:
+            pair = pack_hi.at[a:b], recv_hi.at[1 - dx, a:b]
+        return remote(*pair, send_f.at[g], got_f.at[g], at(dx, dy, 0))
+
+    def edge_copy(dx, dy, dz):
+        a, b = {-1: (0, 128), 0: (0, 256), 1: (128, 256)}[dx]
+        g = group_of(-dx, -dy)
+        if dz == 1:
+            pair = pack_z_lo.at[:, a:b], recv_z_lo.at[g, :, a:b]
+        else:
+            pair = pack_z_hi.at[:, a:b], recv_z_hi.at[g, :, a:b]
+        side = (1 - dz) // 2
+        return remote(*pair, send_z.at[side], got_z.at[side], at(dx, dy, dz))
 
     for dx, dy in GROUPS:
         if (dx, dy) != (0, 0):
             halo_copy(dx, dy).start()
     for dx, dy, dz in NEIGHBOURS:
+        if dz:
+            edge_copy(dx, dy, dz).start()
+    for dx, dy, dz in NEIGHBOURS:
         back = slot_of(-dx, -dy, -dz)
-        if dz:
-            remote(
-                pack_z, recv_z.at[group_of(-dx, -dy) * 2 + DZS.index(-dz)], send_z, got_z, at(dx, dy, dz)
-            ).start()
         remote(mark_own, marks.at[back], send_m, got_m, at(dx, dy, dz)).start()
 
-    table_h[...] = jnp.zeros(table_h.shape, BF16)
-    table_l[...] = jnp.zeros(table_l.shape, BF16)
     own_h[...] = jnp.zeros(own_h.shape, BF16)
     own_l[...] = jnp.zeros(own_l.shape, BF16)
     ztile[...] = jnp.zeros(ztile.shape, F32)
-    main[:, :, 8:16] = jnp.zeros((4, WX, 8, CZ), F32)
-    halo[:, :, 8:16] = jnp.zeros((4, WX, 8, CZ), F32)
+    columns[...] = jnp.zeros(columns.shape, F32)
+    main[:, :, 8:16] = jnp.zeros((WX, 4, 8, CZ), F32)
+    halo[:, :, 8:16] = jnp.zeros((WX, 4, 8, CZ), F32)
     grid[...] = jnp.zeros(grid.shape, F32)
+    edges[...] = jnp.zeros(edges.shape, F32)
     vecs[...] = jnp.zeros(vecs.shape, F32)
 
     live = (lax.broadcasted_iota(jnp.int32, (1, CAP), 1) < counts_ref[0]).astype(F32)
@@ -174,50 +208,67 @@
         y0, ny = ROWS[dy]
         table_x = axis_table(x0, 16, mark[0:1] + float(1 + CX * dx), of(0))
         table_y = axis_table(y0, ny, mark[1:2] + float(1 + CY * dy), of(1))
-        lanes = slice(j * CAP, (j + 1) * CAP)
         for x in range(nx):
-            at_row = STARTS[g] + x * ny
-            wxy[at_row : at_row + ny, lanes] = table_x[x : x + 1] * table_y
-        z0, nz = {-1: (0, 16), 0: (0, TZ), 1: (CZ, 16)}[dz]
-        high, low = split(axis_table(z0, nz, mark[2:3] + float(1 + CZ * dz), of(2)))
-        table_h[g, z0 : z0 + nz, lanes] = high
-        table_l[g, z0 : z0 + nz, lanes] = low
-        if g == CENTRE and dz == 0:
-            own_h[0:TZ] = high
-            own_l[0:TZ] = low
+            rows = slice(STARTS[g] + x * ny, STARTS[g] + (x + 1) * ny)
+            weight = table_x[x : x + 1] * table_y
+            if dz == 0:
+                wxy[rows] = weight
+            else:
+                high, low = split(weight)
+                wxy_h[j, rows] = high
+                wxy_l[j, rows] = low
+        start = mark[2:3] + float(1 + CZ * dz)
+        if dz == 0:
+            high, low = split(axis_table(0, TZ, start, of(2)))
+            table_h[g] = high
+            table_l[g] = low
+            if g == CENTRE:
+                own_h[0:TZ] = high
+                own_l[0:TZ] = low
+        else:
+            touched = axis_table({-1: 0, 1: CZ + 1}[dz], 8, start, of(2))[0:4]
+            edge_w[2 * g + j, 0:12] = jnp.concatenate([touched] * 3, axis=0)
+            edge_w[2 * g + j, 12:16] = jnp.zeros((4, CAP), F32)
 
     build(CENTRE, 2)
 
     for g, (dx, dy) in enumerate(GROUPS):
         if g != CENTRE:
             halo_copy(-dx, -dy).wait_recv()
-    drain(recv_z, got_z)
-    low_rows = lax.broadcasted_iota(jnp.int32, (8, 4 * CX * CY), 0) < 2
+    drain(recv_z_lo.at[0:6], got_z.at[0])
+    drain(recv_z_hi.at[0:6], got_z.at[1])
     for g, (dx, dy) in enumerate(GROUPS):
         (xa, xb), (ya, yb) = TAKE[dx], TAKE[dy]
         x0, y0 = xa + CX * dx + 2, ya + CY * dy + 2
-        source = field if g == CENTRE else recv_f.at[g]
-        main[:, x0 : x0 + xb - xa, y0 : y0 + yb - ya] = source[:, xa:xb, ya:yb]
-        columns = jnp.where(low_rows, recv_z[2 * g], recv_z[2 * g + 1])
-        ztile[:, :, :, 0:8] = columns.T.reshape(4, CX, CY, 8)
-        halo[:, x0 : x0 + xb - xa, y0 : y0 + yb - ya] = ztile[:, xa:xb, ya:yb]
+        planes = slice(x0, x0 + xb - xa)
+        if g == CENTRE:
+            main[planes, :, y0 : y0 + CY] = field[...]
+        elif dy == 0:
+            main[planes, :, y0 : y0 + CY] = recv_x[dx == 1 and 1 or 0, xa:xb]
+        else:
+            source, step = (recv_lo, 2) if dy == -1 else (recv_hi, 4)
+            for c in range(4):
+                main[planes, c, y0 : y0 + yb - ya] = source[
+                    dx + 1, xa:xb, c * step : c * step + yb - ya
+                ]
+        columns[0:2] = recv_z_lo[g]
+        columns[2:6] = recv_z_hi[g]
+        ztile[:, :, :, 0:8] = columns[...].T.reshape(CX, 4, CY, 8)
+        halo[planes, :, y0 : y0 + yb - ya] = ztile[xa:xb, :, ya:yb]
     lane = lax.broadcasted_iota(jnp.int32, (WY, CZ), 1)
 
-    def widen(x, carry):
+    for x in range(WX):
         for c in range(4):
-            turned = pltpu.roll(main[c, x], 2, 1)
-            edge = halo[c, x]
+            turned = pltpu.roll(main[x, c], 2, 1)
+            edge = halo[x, c]
             wide[c, x, :, 0:CZ] = jnp.where(lane < 2, edge, turned)
             wide[c, x, :, CZ:] = jnp.where(lane < 2, turned, jnp.where(lane < 5, edge, 0.0))
-        return carry
-
-    lax.fori_loop(0, WX, widen, 0)
 
     def interpolate():
         high = vel_h[...].reshape(3 * 11 * WY, WZ)
         low = vel_l[...].reshape(3 * 11 * WY, WZ)
         rows = dot3(high, low, own_h[...], own_l[...], ((1,), (0,)))
-        weight = wxy[STARTS[CENTRE] : STARTS[CENTRE] + 11 * WY, 2 * CAP : 3 * CAP]
+        weight = wxy[STARTS[CENTRE] : STARTS[CENTRE] + 11 * WY]
         return [
             jnp.sum(rows[c * 11 * WY : (c + 1) * 11 * WY] * weight, axis=0, keepdims=True)
             for c in range(3)
@@ -240,31 +291,48 @@
             ).start()
         recv_v[a, slot_of(0, 0, 0)] = vecs[a]
 
+    part_row = lax.broadcasted_iota(jnp.int32, (16, CAP), 0)
+
+    def spread_inner(a, g):
+        span = SPANS[g]
+        vector = recv_v[a, 3 * g + 2]
+        weight = wxy[STARTS[g] : STARTS[g] + span]
+        for c in range(3):
+            high, low = split(weight * vector[c : c + 1])
+            left_h[c * span : (c + 1) * span] = high
+            left_l[c * span : (c + 1) * span] = low
+        return dot3(left_h[0 : 3 * span], left_l[0 : 3 * span], table_h[g], table_l[g], ((1,), (1,)))
+
+    def spread_edges(a, g):
+        rows = slice(STARTS[g], STARTS[g] + SPANS[g])
+        sides = []
+        for j in range(2):
+            vector = recv_v[a, 3 * g + j]
+            value = jnp.where(
+                part_row < 4, vector[0:1], jnp.where(part_row < 8, vector[1:2], vector[2:3])
+            )
+            high, low = split(edge_w[2 * g + j] * value)
+            sides.append(dot3(high, low, wxy_h[j, rows], wxy_l[j, rows], ((1,), (1,))))
+        return jnp.concatenate(sides, axis=0).T
+
     def spread(a):
         grid[:, :, :, 0:TZ] = jnp.zeros((3, WX, WY, TZ), F32)
+        edges[:, :, 0:32] = jnp.zeros((WX, WY, 32), F32)
         for g in ORDER:
             (dx, dy) = GROUPS[g]
+            span = SPANS[g]
+            x0, nx = PLANES[dx]
+            y0, ny = ROWS[dy]
             if g == CENTRE:
+                total = spread_inner(a, g)
                 drain(recv_v.at[a, 3 * g : 3 * g + 2], got_v.at[a, g])
             else:
                 drain(recv_v.at[a, 3 * g : 3 * g + 3], got_v.at[a, g])
-            span = SPANS[g]
-            for j in range(3):
-                lanes = slice(j * CAP, (j + 1) * CAP)
-                vector = recv_v[a, 3 * g + j]
-                weight = wxy[STARTS[g] : STARTS[g] + span, lanes]
-                for c in range(3):
-                    high, low = split(weight * vector[c : c + 1])
-                    left_h[c * span : (c + 1) * span, lanes] = high
-                    left_l[c * span : (c + 1) * span, lanes] = low
-            total = dot3(
-                left_h[0 : 3 * span], left_l[0 : 3 * span], table_h[g], table_l[g], ((1,), (1,))
-            )
-            x0, nx = PLANES[dx]
-            y0, ny = ROWS[dy]
+                total = spread_inner(a, g)
             for c in range(3):
                 at_place = (c, slice(x0, x0 + nx), slice(y0, y0 + ny), slice(0, TZ))
                 grid[at_place] += total[c * span : (c + 1) * span].reshape(nx, ny, TZ)
+            edges[x0 : x0 + nx, y0 : y0 + ny, 0:32] += spread_edges(a, g).reshape(nx, ny, 32)
 
     def shifts(value, axis):
         length = value.shape[axis]
@@ -275,9 +343,19 @@
         return before + after
 
     def stream():
-        def planes(x, carry):
+        for x in range(WX):
             scale = wide[3, x]
-            m0, m1, m2 = (scale * grid[c, x] for c in range(3))
+            edge = edges[x]
+            values = []
+            for c in range(3):
+                head = grid[c, x, :, 0:CZ] + jnp.where(
+                    lane < 4, pltpu.roll(edge, CZ - 4 * c, 1) if c else edge, 0.0
+                )
+                tail = grid[c, x, :, CZ:] + jnp.where(
+                    (lane > 0) & (lane < 5), pltpu.roll(edge, CZ - 15 - 4 * c, 1), 0.0
+                )
+                values.append(scale * jnp.concatenate([head, tail], axis=1))
+            m0, m1, m2 = values
             moved[0, x], moved[1, x], moved[2, x] = m0, m1, m2
             before, after = shifts(m0, 0)
             sy0, dy0 = before + after, before - after
@@ -299,22 +377,21 @@
             plane_a[2, x] = sz2
             plane_b[2, x] = dz0
             plane_c[1, x] = 2.0 * sz2 + both(sz2, 0) + dyz1
-            return carry
-
-        lax.fori_loop(0, WX, planes, 0)
-
-        def velocity(x, carry):
+
+        energy = jnp.zeros((WY, WZ), F32)
+        for x in range(1, 12):
             half = wide[3, x] * 0.5
             for c in range(3):
                 post = plane_a[c, x - 1] + plane_a[c, x + 1] + plane_b[c, x - 1] - plane_b[c, x + 1]
                 if c:
                     post = post + plane_c[c - 1, x]
-                high, low = split(half * (moved[c, x] + post * (1.0 / 12.0)))
+                response = moved[c, x] + post * (1.0 / 12.0)
+                high, low = split(half * response)
                 vel_h[c, x - 1] = high
                 vel_l[c, x - 1] = low
-            return carry
-
-        lax.fori_loop(1, 12, velocity, 0)
+                if 2 <= x < 2 + CX:
+                    energy = energy + moved[c, x] * response
+        energy_ref[...] = energy
 
     def apply(a, carry):
         send_vector(a)
@@ -328,22 +405,33 @@
 
         spread(a)
         stream()
-        for c, value in enumerate(interpolate()):
-            vector = vecs[a, c : c + 1]
-            image = live * (value + stiff * vector)
-            images[a, c : c + 1] = image
-            vecs[a + 1, c : c + 1] = image - SHIFT * vector
+
+        @pl.when(a < ITERS - 1)
+        def _():
+            for c, value in enumerate(interpolate()):
+                vector = vecs[a, c : c + 1]
+                image = live * (value + stiff * vector)
+                images[a, c : c + 1] = image
+                vecs[a + 1, c : c + 1] = image - SHIFT * vector
+
         return carry
 
     lax.fori_loop(0, ITERS, apply, 0)
 
     lane_row = lax.broadcasted_iota(jnp.int32, (1, 128), 1)
     v = [vecs[k, 0:3] for k in range(3)]
-    w = [images[k, 0:3] for k in range(3)]
-    pairs = [(v[i], w[j]) for i in range(3) for j in range(i, 3)] + [(v[0], v[j]) for j in range(3)]
+    w = [images[k, 0:3] for k in range(2)]
+    inside = lambda axis, size: (
+        lax.broadcasted_iota(jnp.int32, (WY, WZ), axis) - 2
+    ).astype(jnp.uint32) < size
+    energy = jnp.where(inside(0, CY) & inside(1, CZ), energy_ref[...], 0.0)
+    last = 0.5 * jnp.sum(energy) + jnp.sum(stiff * v[2] * v[2])
+    pairs = [(v[0], w[0]), (v[0], w[1]), (v[2], w[0]), (v[1], w[1]), (v[2], w[1])]
+    pairs = pairs + [(v[0], v[j]) for j in range(3)]
     row = jnp.zeros((1, 128), F32)
     for k, (left, right) in enumerate(pairs):
         row = jnp.where(lane_row == k, jnp.sum(left * right), row)
+    row = jnp.where(lane_row == len(pairs), last, row)
     me = iy * size_z + iz
     part[...] = row
     recv_a[me] = row
@@ -361,7 +449,7 @@
         remote(part_b, recv_b.at[ix], send_r.at[1], got_r.at[1], along(k)).start()
     drain(recv_b.at[0 : size_x - 1], got_r.at[1])
     total = jnp.sum(recv_b[...], axis=0)
-    h00, h01, h02, h11, h12, h22, b0, b1, b2 = (
+    h00, h01, h02, h11, h12, b0, b1, b2, h22 = (
         jnp.sum(jnp.where(lane_row == k, total, 0.0), axis=1, keepdims=True) for k in range(9)
     )
 
@@ -385,7 +473,8 @@
     for dx, dy in GROUPS:
         if (dx, dy) != (0, 0):
             halo_copy(dx, dy).wait_send()
-    drain(recv_z, send_z)
+    drain(recv_z_lo.at[0:6], send_z.at[0])
+    drain(recv_z_hi.at[0:6], send_z.at[1])
     drain(marks.at[0:26], send_m)
     for a in range(ITERS):
         drain(recv_v.at[a, 0:26], send_v.at[a])
@@ -402,34 +491,51 @@
         return pl.pallas_call(
             functools.partial(kernel, sizes),
             out_shape=jax.ShapeDtypeStruct((3, CAP), F32),
-            in_specs=[vmem] * 6 + [pl.BlockSpec(memory_space=pltpu.SMEM)],
+            in_specs=[pl.BlockSpec(memory_space=pl.ANY)] * 6 + [pl.BlockSpec(memory_space=pltpu.SMEM)],
             out_specs=vmem,
             scratch_shapes=[
-                pltpu.VMEM((4, CX, CY, CZ), F32),
+                pltpu.VMEM((CX, CY, CZ), F32),
+                pltpu.VMEM((3, CAP), jnp.int32),
+                pltpu.VMEM((3, CAP), F32),
+                pltpu.VMEM((3, CAP), F32),
+                pltpu.VMEM((1, CAP), F32),
+                pltpu.VMEM((CX, 4, CY, CZ), F32),
                 pltpu.VMEM((CZ, 4 * CX * CY), F32),
+                pltpu.VMEM((CX, 8, CZ), F32),
+                pltpu.VMEM((CX, 16, CZ), F32),
+                pltpu.VMEM((2, 4 * CX * CY), F32),
+                pltpu.VMEM((4, 4 * CX * CY), F32),
+                pltpu.VMEM((8, CAP), F32),
+                pltpu.VMEM((2, CX, 4, CY, CZ), F32),
+                pltpu.VMEM((3, CX, 8, CZ), F32),
+                pltpu.VMEM((3, CX, 16, CZ), F32),
+                pltpu.VMEM((9, 2, 4 * CX * CY), F32),
+                pltpu.VMEM((9, 4, 4 * CX * CY), F32),
                 pltpu.VMEM((8, 4 * CX * CY), F32),
-                pltpu.VMEM((8, CAP), F32),
-                pltpu.VMEM((9, 4, CX, CY, CZ), F32),
-                pltpu.VMEM((18, 8, 4 * CX * CY), F32),
                 pltpu.VMEM((27, 8, CAP), F32),
-                pltpu.VMEM((4, WX, WY, CZ), F32),
-                pltpu.VMEM((4, WX, WY, CZ), F32),
-                pltpu.VMEM((4, CX, CY, CZ), F32),
+                pltpu.VMEM((WX, 4, WY, CZ), F32),
+                pltpu.VMEM((WX, 4, WY, CZ), F32),
+                pltpu.VMEM((CX, 4, CY, CZ), F32),
                 pltpu.VMEM((4, WX, WY, WZ), F32),
-                pltpu.VMEM((9, TZ, 3 * CAP), BF16),
-                pltpu.VMEM((9, TZ, 3 * CAP), BF16),
+                pltpu.VMEM((9, TZ, CAP), BF16),
+                pltpu.VMEM((9, TZ, CAP), BF16),
                 pltpu.VMEM((WZ, CAP), BF16),
                 pltpu.VMEM((WZ, CAP), BF16),
-                pltpu.VMEM((sum(SPANS), 3 * CAP), F32),
-                pltpu.VMEM((3 * max(SPANS), 3 * CAP), BF16),
-                pltpu.VMEM((3 * max(SPANS), 3 * CAP), BF16),
+                pltpu.VMEM((sum(SPANS), CAP), F32),
+                pltpu.VMEM((2, sum(SPANS), CAP), BF16),
+                pltpu.VMEM((2, sum(SPANS), CAP), BF16),
+                pltpu.VMEM((18, 16, CAP), F32),
+                pltpu.VMEM((3 * max(SPANS), CAP), BF16),
+                pltpu.VMEM((3 * max(SPANS), CAP), BF16),
                 pltpu.VMEM((3, WX, WY, WZ), F32),
+                pltpu.VMEM((WX, WY, CZ), F32),
                 pltpu.VMEM((3, WX, WY, WZ), F32),
                 pltpu.VMEM((3, WX, WY, WZ), F32),
                 pltpu.VMEM((3, WX, WY, WZ), F32),
                 pltpu.VMEM((2, WX, WY, WZ), F32),
                 pltpu.VMEM((3, 11, WY, WZ), BF16),
                 pltpu.VMEM((3, 11, WY, WZ), BF16),
+                pltpu.VMEM((WY, WZ), F32),
                 pltpu.VMEM((ITERS + 1, 4, CAP), F32),
                 pltpu.VMEM((ITERS, 4, CAP), F32),
                 pltpu.VMEM((ITERS, 27, 4, CAP), F32),
@@ -437,10 +543,11 @@
                 pltpu.VMEM((plane, 1, 128), F32),
                 pltpu.VMEM((1, 128), F32),
                 pltpu.VMEM((sizes[0], 1, 128), F32),
+                pltpu.SemaphoreType.DMA((8,)),
                 pltpu.SemaphoreType.DMA((9,)),
                 pltpu.SemaphoreType.DMA((9,)),
-                pltpu.SemaphoreType.DMA,
-                pltpu.SemaphoreType.DMA,
+                pltpu.SemaphoreType.DMA((2,)),
+                pltpu.SemaphoreType.DMA((2,)),
                 pltpu.SemaphoreType.DMA,
                 pltpu.SemaphoreType.DMA,
                 pltpu.SemaphoreType.DMA((ITERS,)),

time: 69.4 us -> 53.5 us (0.77)
  Pallas kernels: 67.3 us -> 51.4 us
    pallas_call x1, Pallas kernels: 67.3 us -> 51.4 us  [body(): pl.pallas_call(functools.partial(kernel, sizes), out_shape=jax.ShapeDtype...]
where the time goes in v2:
time: 53.5 us; the launch traced here: 53.4 us
  Pallas kernels  51.4 us (96%)
  local copies, waits for them, and re-layouts  1.28 us (2%)
  between operations  0.66 us (1%)
    pallas_call x1, Pallas kernels, body(): pl.pallas_call(functools.partial(kernel, sizes), out_shape=jax.ShapeDtype...  51.4 us
    unnamed x1, local copies, waits for them, and re-layouts  1.28 us

profile of v2, /device:TPU:1, one launch (start us, length us, event | category | flops | bytes accessed | tf_op | source)
XLA Modules:
  0.0 53.4 jit_solution(6781273975110827206)
XLA Ops:
  0.7 51.4 %immersed.1 = f32[3,256]{1,0:T(4,128)} custom-call(f32[8,8,128]{2,1,0:T(8,128)} %density_in.1, f32[3,8,8,128]{3,2,1,0:T(8,128)} %base_in.1, s32[3,256]{1,0:T(4,128)} %cells_in.1, f32[3,256]{1,0:T(4,128)} %offsets_in.1, f32[3,256]{1,0:T(4,128)} %target_in.1, f32[1,256]{1,0:T(1,128)} %bitcast.1, s32[1]{0:T(128)S(6)} %copy.9.counts_ref), custom_call_target="tpu_custom_call" | custom-call | tf_op jit(solution)/shard_map/immersed/pallas_call | solution.py:491
  52.1 1.3 %copy.10 = f32[3,256]{1,0:T(4,128)} copy(f32[3,256]{1,0:T(4,128)} %immersed.1) | data formatting | bytes 6144

commit v3 on v2

--- a/solution.py
+++ b/solution.py
@@ -59,13 +59,14 @@
 
 def kernel(
     sizes,
-    density_in, base_in, cells_in, offsets_in, target_in, stiff_in, counts_ref,
+    density_in, base_in, cells_in, offsets_in, target_in, stiff_in, counts_in,
     out_ref,
+    counts_ref,
     density_ref, cells_ref, offsets_ref, target_ref, stiff_ref,
     field, ftrans, pack_lo, pack_hi, pack_z_lo, pack_z_hi, mark_own, recv_x, recv_lo, recv_hi,
     recv_z_lo, recv_z_hi, columns, marks, main, halo, ztile, wide,
     table_h, table_l, own_h, own_l, wxy, wxy_h, wxy_l, edge_w, left_h, left_l, grid, edges, moved, plane_a, plane_b, plane_c,
-    vel_h, vel_l, energy_ref, vecs, images, recv_v, part, recv_a, part_b, recv_b,
+    vel_h, vel_l, vecs, images, recv_v, part, recv_a, part_b, recv_b,
     loaded, send_f, got_f, send_z, got_z, send_m, got_m, send_v, got_v, send_r, got_r,
 ):
     size_x, size_y, size_z = sizes
@@ -93,7 +94,7 @@
         for k, (source, target) in enumerate(
             [
                 (density_in, density_ref), (cells_in, cells_ref), (offsets_in, offsets_ref),
-                (target_in, target_ref), (stiff_in, stiff_ref),
+                (target_in, target_ref), (stiff_in, stiff_ref), (counts_in, counts_ref),
             ]
         )
     ]
@@ -281,13 +282,12 @@
     for c, value in enumerate(interpolate()):
         vecs[0, c : c + 1] = live * (target_ref[c : c + 1] - value)
 
-    drain(marks.at[0:26], got_m)
-
     def send_vector(a):
         for dx, dy, dz in NEIGHBOURS:
             back = slot_of(-dx, -dy, -dz)
             remote(
-                vecs.at[a], recv_v.at[a, back], send_v.at[a], got_v.at[a, back // 3], at(dx, dy, dz)
+                vecs.at[a], recv_v.at[a, back], send_v.at[a], got_v.at[a, abs(dx) + abs(dy) + abs(dz) - 1],
+                at(dx, dy, dz),
             ).start()
         recv_v[a, slot_of(0, 0, 0)] = vecs[a]
 
@@ -315,24 +315,34 @@
             sides.append(dot3(high, low, wxy_h[j, rows], wxy_l[j, rows], ((1,), (1,))))
         return jnp.concatenate(sides, axis=0).T
 
+    def add_inner(a, g):
+        (dx, dy), span = GROUPS[g], SPANS[g]
+        x0, nx = PLANES[dx]
+        y0, ny = ROWS[dy]
+        total = spread_inner(a, g)
+        for c in range(3):
+            at_place = (c, slice(x0, x0 + nx), slice(y0, y0 + ny), slice(0, TZ))
+            grid[at_place] += total[c * span : (c + 1) * span].reshape(nx, ny, TZ)
+
+    def add_edges(a, g):
+        dx, dy = GROUPS[g]
+        x0, nx = PLANES[dx]
+        y0, ny = ROWS[dy]
+        edges[x0 : x0 + nx, y0 : y0 + ny, 0:32] += spread_edges(a, g).reshape(nx, ny, 32)
+
     def spread(a):
+        far = [abs(dx) + abs(dy) for dx, dy in GROUPS]
         grid[:, :, :, 0:TZ] = jnp.zeros((3, WX, WY, TZ), F32)
         edges[:, :, 0:32] = jnp.zeros((WX, WY, 32), F32)
-        for g in ORDER:
-            (dx, dy) = GROUPS[g]
-            span = SPANS[g]
-            x0, nx = PLANES[dx]
-            y0, ny = ROWS[dy]
-            if g == CENTRE:
-                total = spread_inner(a, g)
-                drain(recv_v.at[a, 3 * g : 3 * g + 2], got_v.at[a, g])
-            else:
-                drain(recv_v.at[a, 3 * g : 3 * g + 3], got_v.at[a, g])
-                total = spread_inner(a, g)
-            for c in range(3):
-                at_place = (c, slice(x0, x0 + nx), slice(y0, y0 + ny), slice(0, TZ))
-                grid[at_place] += total[c * span : (c + 1) * span].reshape(nx, ny, TZ)
-            edges[x0 : x0 + nx, y0 : y0 + ny, 0:32] += spread_edges(a, g).reshape(nx, ny, 32)
+        for hops, messages in enumerate((0, 6, 12, 8)):
+            if hops:
+                drain(recv_v.at[a, 0:messages], got_v.at[a, hops - 1])
+            for g in range(9):
+                if far[g] == hops:
+                    add_inner(a, g)
+            for g in range(9):
+                if far[g] == hops - 1:
+                    add_edges(a, g)
 
     def shifts(value, axis):
         length = value.shape[axis]
@@ -342,8 +352,8 @@
         before, after = shifts(value, axis)
         return before + after
 
-    def stream():
-        for x in range(WX):
+    def stream(last):
+        for x in range(1, 11) if last else range(WX):
             scale = wide[3, x]
             edge = edges[x]
             values = []
@@ -379,78 +389,84 @@
             plane_c[1, x] = 2.0 * sz2 + both(sz2, 0) + dyz1
 
         energy = jnp.zeros((WY, WZ), F32)
-        for x in range(1, 12):
+        for x in range(2, 10) if last else range(1, 12):
             half = wide[3, x] * 0.5
             for c in range(3):
                 post = plane_a[c, x - 1] + plane_a[c, x + 1] + plane_b[c, x - 1] - plane_b[c, x + 1]
                 if c:
                     post = post + plane_c[c - 1, x]
                 response = moved[c, x] + post * (1.0 / 12.0)
-                high, low = split(half * response)
-                vel_h[c, x - 1] = high
-                vel_l[c, x - 1] = low
-                if 2 <= x < 2 + CX:
+                if last:
                     energy = energy + moved[c, x] * response
-        energy_ref[...] = energy
-
-    def apply(a, carry):
+                else:
+                    high, low = split(half * response)
+                    vel_h[c, x - 1] = high
+                    vel_l[c, x - 1] = low
+        return energy
+
+    lane_row = lax.broadcasted_iota(jnp.int32, (1, 128), 1)
+    me = iy * size_z + iz
+    mates = size_y * size_z - 1
+
+    def sum_plane(k, row):
+        part[k] = row
+        recv_a[k, me] = row
+        for other in range(1, mates + 1):
+            remote(part.at[k], recv_a.at[k, me], send_r.at[k], got_r.at[k], mate(other)).start()
+
+    def sum_along(k):
+        drain(recv_a.at[k, 0:mates], got_r.at[k])
+        row = jnp.sum(recv_a[k], axis=0)
+        part_b[k] = row
+        recv_b[k, ix] = row
+        for other in range(1, size_x):
+            remote(
+                part_b.at[k], recv_b.at[k, ix], send_r.at[2 + k], got_r.at[2 + k], along(other)
+            ).start()
+
+    def summed(k):
+        drain(recv_b.at[k, 0 : size_x - 1], got_r.at[2 + k])
+        return jnp.sum(recv_b[k], axis=0)
+
+    for a in range(ITERS):
         send_vector(a)
-
-        @pl.when(a == 0)
-        def _():
+        if a == 0:
+            drain(marks.at[0:26], got_m)
             for g in ORDER:
                 for j in range(3):
                     if (g, j) != (CENTRE, 2):
                         build(g, j)
-
+        last = a == ITERS - 1
+        if last:
+            v = [vecs[k, 0:3] for k in range(3)]
+            w = [images[k, 0:3] for k in range(2)]
+            pairs = [(v[0], w[0]), (v[0], w[1]), (v[2], w[0]), (v[1], w[1]), (v[2], w[1])]
+            pairs = pairs + [(v[0], v[j]) for j in range(3)]
+            row = jnp.zeros((1, 128), F32)
+            for k, (left, right) in enumerate(pairs):
+                row = jnp.where(lane_row == k, jnp.sum(left * right), row)
+            sum_plane(0, row)
         spread(a)
-        stream()
-
-        @pl.when(a < ITERS - 1)
-        def _():
+        if last:
+            sum_along(0)
+        energy = stream(last)
+        if not last:
             for c, value in enumerate(interpolate()):
                 vector = vecs[a, c : c + 1]
                 image = live * (value + stiff * vector)
                 images[a, c : c + 1] = image
                 vecs[a + 1, c : c + 1] = image - SHIFT * vector
 
-        return carry
-
-    lax.fori_loop(0, ITERS, apply, 0)
-
-    lane_row = lax.broadcasted_iota(jnp.int32, (1, 128), 1)
-    v = [vecs[k, 0:3] for k in range(3)]
-    w = [images[k, 0:3] for k in range(2)]
     inside = lambda axis, size: (
         lax.broadcasted_iota(jnp.int32, (WY, WZ), axis) - 2
     ).astype(jnp.uint32) < size
-    energy = jnp.where(inside(0, CY) & inside(1, CZ), energy_ref[...], 0.0)
-    last = 0.5 * jnp.sum(energy) + jnp.sum(stiff * v[2] * v[2])
-    pairs = [(v[0], w[0]), (v[0], w[1]), (v[2], w[0]), (v[1], w[1]), (v[2], w[1])]
-    pairs = pairs + [(v[0], v[j]) for j in range(3)]
-    row = jnp.zeros((1, 128), F32)
-    for k, (left, right) in enumerate(pairs):
-        row = jnp.where(lane_row == k, jnp.sum(left * right), row)
-    row = jnp.where(lane_row == len(pairs), last, row)
-    me = iy * size_z + iz
-    part[...] = row
-    recv_a[me] = row
-
-    def send_mate(k, carry):
-        remote(part, recv_a.at[me], send_r.at[0], got_r.at[0], mate(k)).start()
-        return carry
-
-    lax.fori_loop(1, size_y * size_z, send_mate, 0)
-    drain(recv_a.at[0 : size_y * size_z - 1], got_r.at[0])
-    total = jnp.sum(recv_a[...], axis=0)
-    part_b[...] = total
-    recv_b[ix] = total
-    for k in range(1, size_x):
-        remote(part_b, recv_b.at[ix], send_r.at[1], got_r.at[1], along(k)).start()
-    drain(recv_b.at[0 : size_x - 1], got_r.at[1])
-    total = jnp.sum(recv_b[...], axis=0)
-    h00, h01, h02, h11, h12, b0, b1, b2, h22 = (
-        jnp.sum(jnp.where(lane_row == k, total, 0.0), axis=1, keepdims=True) for k in range(9)
+    energy = jnp.where(inside(0, CY) & inside(1, CZ), energy, 0.0)
+    own = jnp.sum(0.5 * energy, axis=0, keepdims=True)
+    own = own + jnp.sum(stiff * v[2] * v[2], axis=0, keepdims=True)
+    sum_plane(1, own[:, 0:128] + own[:, 128:256])
+    total = summed(0)
+    h00, h01, h02, h11, h12, b0, b1, b2 = (
+        jnp.sum(jnp.where(lane_row == k, total, 0.0), axis=1, keepdims=True) for k in range(8)
     )
 
     def over(top, pivot, size):
@@ -462,13 +478,16 @@
     d1 = h11 - l10 * h01
     e12 = h12 - l10 * h02
     l21 = over(e12, d1, h11)
-    d2 = h22 - l20 * h02 - l21 * e12
+    less = h02 * l20 + l21 * e12
     z1 = b1 - l10 * b0
     z2 = b2 - l20 * b0 - l21 * z1
-    y2 = over(z2, d2, h22)
-    y1 = over(z1, d1, h11) - l21 * y2
-    y0 = over(b0, h00, h00) - l10 * y1 - l20 * y2
-    out_ref[...] = y0 * v[0] + y1 * v[1] + y2 * v[2]
+    y1 = over(z1, d1, h11)
+    y0 = over(b0, h00, h00) - l10 * y1
+    first = y0 * v[0] + y1 * v[1]
+    second = v[2] - l21 * v[1] + (l10 * l21 - l20) * v[0]
+    sum_along(1)
+    h22 = jnp.sum(summed(1), axis=1, keepdims=True)
+    out_ref[...] = first + over(z2, h22 - less, h22) * second
 
     for dx, dy in GROUPS:
         if (dx, dy) != (0, 0):
@@ -478,8 +497,9 @@
     drain(marks.at[0:26], send_m)
     for a in range(ITERS):
         drain(recv_v.at[a, 0:26], send_v.at[a])
-    drain(recv_a.at[0 : size_y * size_z - 1], send_r.at[0])
-    drain(recv_b.at[0 : size_x - 1], send_r.at[1])
+    for k in range(2):
+        drain(recv_a.at[k, 0:mates], send_r.at[k])
+        drain(recv_b.at[k, 0 : size_x - 1], send_r.at[2 + k])
 
 
 def solution(mesh):
@@ -491,9 +511,10 @@
         return pl.pallas_call(
             functools.partial(kernel, sizes),
             out_shape=jax.ShapeDtypeStruct((3, CAP), F32),
-            in_specs=[pl.BlockSpec(memory_space=pl.ANY)] * 6 + [pl.BlockSpec(memory_space=pltpu.SMEM)],
+            in_specs=[pl.BlockSpec(memory_space=pl.ANY)] * 7,
             out_specs=vmem,
             scratch_shapes=[
+                pltpu.SMEM((1,), jnp.int32),
                 pltpu.VMEM((CX, CY, CZ), F32),
                 pltpu.VMEM((3, CAP), jnp.int32),
                 pltpu.VMEM((3, CAP), F32),
@@ -535,15 +556,14 @@
                 pltpu.VMEM((2, WX, WY, WZ), F32),
                 pltpu.VMEM((3, 11, WY, WZ), BF16),
                 pltpu.VMEM((3, 11, WY, WZ), BF16),
-                pltpu.VMEM((WY, WZ), F32),
                 pltpu.VMEM((ITERS + 1, 4, CAP), F32),
                 pltpu.VMEM((ITERS, 4, CAP), F32),
                 pltpu.VMEM((ITERS, 27, 4, CAP), F32),
-                pltpu.VMEM((1, 128), F32),
-                pltpu.VMEM((plane, 1, 128), F32),
-                pltpu.VMEM((1, 128), F32),
-                pltpu.VMEM((sizes[0], 1, 128), F32),
-                pltpu.SemaphoreType.DMA((8,)),
+                pltpu.VMEM((2, 1, 128), F32),
+                pltpu.VMEM((2, plane, 1, 128), F32),
+                pltpu.VMEM((2, 1, 128), F32),
+                pltpu.VMEM((2, sizes[0], 1, 128), F32),
+                pltpu.SemaphoreType.DMA((9,)),
                 pltpu.SemaphoreType.DMA((9,)),
                 pltpu.SemaphoreType.DMA((9,)),
                 pltpu.SemaphoreType.DMA((2,)),
@@ -551,9 +571,9 @@
                 pltpu.SemaphoreType.DMA,
                 pltpu.SemaphoreType.DMA,
                 pltpu.SemaphoreType.DMA((ITERS,)),
-                pltpu.SemaphoreType.DMA((ITERS, 9)),
-                pltpu.SemaphoreType.DMA((2,)),
-                pltpu.SemaphoreType.DMA((2,)),
+                pltpu.SemaphoreType.DMA((ITERS, 3)),
+                pltpu.SemaphoreType.DMA((4,)),
+                pltpu.SemaphoreType.DMA((4,)),
             ],
             compiler_params=pltpu.CompilerParams(
                 collective_id=0, has_side_effects=True, vmem_limit_bytes=60 * 1024 * 1024

time: 53.5 us -> 48.7 us (0.910)
  Pallas kernels: 51.4 us -> 46.6 us
    pallas_call x1, Pallas kernels: 51.4 us -> 46.6 us  [body(): pl.pallas_call(functools.partial(kernel, sizes), out_shape=jax.ShapeDtype...]
where the time goes in v3:
time: 48.7 us; the launch traced here: 48.6 us
  Pallas kernels  46.6 us (96%)
  local copies, waits for them, and re-layouts  1.28 us (3%)
  between operations  0.66 us (1%)
    pallas_call x1, Pallas kernels, body(): pl.pallas_call(functools.partial(kernel, sizes), out_shape=jax.ShapeDtype...  46.6 us
    unnamed x1, local copies, waits for them, and re-layouts  1.28 us

profile of v3, /device:TPU:1, one launch (start us, length us, event | category | flops | bytes accessed | tf_op | source)
XLA Modules:
  0.0 48.6 jit_solution(4220129449637862060)
XLA Ops:
  0.7 46.6 %immersed.1 = f32[3,256]{1,0:T(4,128)} custom-call(f32[8,8,128]{2,1,0:T(8,128)} %density_in.1, f32[3,8,8,128]{3,2,1,0:T(8,128)} %base_in.1, s32[3,256]{1,0:T(4,128)} %cells_in.1, f32[3,256]{1,0:T(4,128)} %offsets_in.1, f32[3,256]{1,0:T(4,128)} %target_in.1, f32[1,256]{1,0:T(1,128)} %bitcast.1, s32[1]{0:T(128)S(6)} %copy.9.counts_in), custom_call_target="tpu_custom_call" | custom-call | tf_op jit(solution)/shard_map/immersed/pallas_call | solution.py:511
  47.3 1.3 %copy.10 = f32[3,256]{1,0:T(4,128)} copy(f32[3,256]{1,0:T(4,128)} %immersed.1) | data formatting | bytes 6144

commit v4 on v3

--- a/solution.py
+++ b/solution.py
@@ -24,6 +24,10 @@
 PLANES = {-1: (0, 4), 0: (1, 12), 1: (9, 4)}
 ROWS = {-1: (0, 8), 0: (0, 16), 1: (8, 8)}
 TAKE = {-1: (6, 8), 0: (0, 8), 1: (0, 3)}
+TAKE_BASE = {-1: (7, 8), 0: (0, 8), 1: (0, 2)}
+MIDDLE = (5, 6, 7)
+OUTER = (1, 2, 3, 4, 8, 9, 10, 11)
+PLACE = {x: k for k, x in enumerate(OUTER + MIDDLE)}
 
 
 def group_of(dx, dy):
@@ -40,6 +44,7 @@
     for dz in DZS
     if (GROUPS[g][0], GROUPS[g][1], dz) != (0, 0, 0)
 ]
+NEIGHBOURS.sort(key=lambda offset: sum(map(abs, offset)))
 CENTRE = group_of(0, 0)
 SPANS = [PLANES[dx][1] * ROWS[dy][1] for dx, dy in GROUPS]
 STARTS = [sum(SPANS[:g]) for g in range(9)]
@@ -63,11 +68,12 @@
     out_ref,
     counts_ref,
     density_ref, cells_ref, offsets_ref, target_ref, stiff_ref,
-    field, ftrans, pack_lo, pack_hi, pack_z_lo, pack_z_hi, mark_own, recv_x, recv_lo, recv_hi,
+    field, ftrans, pack_lo, pack_hi, spack_lo, spack_hi, pack_z_lo, pack_z_hi, mark_own,
+    recv_x, recv_lo, recv_hi, srecv_x, srecv_lo, srecv_hi,
     recv_z_lo, recv_z_hi, columns, marks, main, halo, ztile, wide,
     table_h, table_l, own_h, own_l, wxy, wxy_h, wxy_l, edge_w, left_h, left_l, grid, edges, moved, plane_a, plane_b, plane_c,
     vel_h, vel_l, vecs, images, recv_v, part, recv_a, part_b, recv_b,
-    loaded, send_f, got_f, send_z, got_z, send_m, got_m, send_v, got_v, send_r, got_r,
+    loaded, send_f, got_f, send_s, got_s, send_z, got_z, send_m, got_m, send_v, got_v, send_r, got_r,
 ):
     size_x, size_y, size_z = sizes
     ix, iy, iz = (lax.axis_index(a) for a in AXES)
@@ -79,9 +85,8 @@
             lax.rem(iz + dz + size_z, size_z),
         )
 
-    def mate(k):
-        rest = lax.rem(iy * size_z + iz + k, size_y * size_z)
-        return (ix, rest // size_z, lax.rem(rest, size_z))
+    def mate(y, z):
+        return (ix, lax.rem(iy + y, size_y), lax.rem(iz + z, size_z))
 
     def along(k):
         return (lax.rem(ix + k, size_x), iy, iz)
@@ -106,7 +111,8 @@
         pl.semaphore_signal(barrier, inc=1, device_id=at(*offset), device_id_type=MESH)
 
     def greet_mate(k, carry):
-        pl.semaphore_signal(barrier, inc=1, device_id=mate(k), device_id_type=MESH)
+        other = mate(k // size_z, lax.rem(k, size_z))
+        pl.semaphore_signal(barrier, inc=1, device_id=other, device_id_type=MESH)
         return carry
 
     lax.fori_loop(1, size_y * size_z, greet_mate, 0)
@@ -119,9 +125,11 @@
     ftrans[...] = field[...].reshape(4 * CX * CY, CZ).T
     pack_z_lo[...] = ftrans[CZ - 2 : CZ]
     pack_z_hi[...] = ftrans[0:4]
-    for c in range(4):
-        pack_lo[:, 2 * c : 2 * c + 2] = field[:, c, CY - 2 : CY]
-        pack_hi[:, 4 * c : 4 * c + 4] = field[:, c, 0:4]
+    for c in range(3):
+        pack_lo[:, c : c + 1] = field[:, c, CY - 1 : CY]
+        pack_hi[:, 2 * c : 2 * c + 2] = field[:, c, 0:2]
+    spack_lo[...] = field[:, 3, CY - 2 : CY]
+    spack_hi[...] = field[:, 3, 0:4]
     anchors = (ix * CX, iy * CY, iz * CZ)
     for k in range(3):
         mark_own[k : k + 1] = (cells_ref[k : k + 1] - anchors[k]).astype(F32)
@@ -141,15 +149,26 @@
         pltpu.make_async_copy(ref, ref, sem).wait()
 
     def halo_copy(dx, dy):
-        a, b = TAKE[-dx]
+        a, b = TAKE_BASE[-dx]
         g = group_of(-dx, -dy)
         if dy == 0:
-            pair = field.at[a:b], recv_x.at[dx == -1 and 1 or 0, a:b]
+            pair = field.at[a:b, 0:3], recv_x.at[(1 - dx) // 2, a:b]
         elif dy == 1:
             pair = pack_lo.at[a:b], recv_lo.at[1 - dx, a:b]
         else:
             pair = pack_hi.at[a:b], recv_hi.at[1 - dx, a:b]
         return remote(*pair, send_f.at[g], got_f.at[g], at(dx, dy, 0))
+
+    def scale_copy(dx, dy):
+        a, b = TAKE[-dx]
+        g = group_of(-dx, -dy)
+        if dy == 0:
+            pair = field.at[a:b, 3], srecv_x.at[(1 - dx) // 2, a:b]
+        elif dy == 1:
+            pair = spack_lo.at[a:b], srecv_lo.at[1 - dx, a:b]
+        else:
+            pair = spack_hi.at[a:b], srecv_hi.at[1 - dx, a:b]
+        return remote(*pair, send_s.at[g], got_s.at[g], at(dx, dy, 0))
 
     def edge_copy(dx, dy, dz):
         a, b = {-1: (0, 128), 0: (0, 256), 1: (128, 256)}[dx]
@@ -161,12 +180,14 @@
         side = (1 - dz) // 2
         return remote(*pair, send_z.at[side], got_z.at[side], at(dx, dy, dz))
 
-    for dx, dy in GROUPS:
-        if (dx, dy) != (0, 0):
-            halo_copy(dx, dy).start()
+    around = [GROUPS[g] for g in reversed(ORDER) if g != CENTRE]
     for dx, dy, dz in NEIGHBOURS:
         if dz:
             edge_copy(dx, dy, dz).start()
+    for dx, dy in around:
+        halo_copy(dx, dy).start()
+    for dx, dy in around:
+        scale_copy(dx, dy).start()
     for dx, dy, dz in NEIGHBOURS:
         back = slot_of(-dx, -dy, -dz)
         remote(mark_own, marks.at[back], send_m, got_m, at(dx, dy, dz)).start()
@@ -175,7 +196,7 @@
     own_l[...] = jnp.zeros(own_l.shape, BF16)
     ztile[...] = jnp.zeros(ztile.shape, F32)
     columns[...] = jnp.zeros(columns.shape, F32)
-    main[:, :, 8:16] = jnp.zeros((WX, 4, 8, CZ), F32)
+    main[...] = jnp.zeros(main.shape, F32)
     halo[:, :, 8:16] = jnp.zeros((WX, 4, 8, CZ), F32)
     grid[...] = jnp.zeros(grid.shape, F32)
     edges[...] = jnp.zeros(edges.shape, F32)
@@ -233,53 +254,69 @@
 
     build(CENTRE, 2)
 
-    for g, (dx, dy) in enumerate(GROUPS):
-        if g != CENTRE:
-            halo_copy(-dx, -dy).wait_recv()
+    lane = lax.broadcasted_iota(jnp.int32, (WY, CZ), 1)
+
+    def place(takes, comps, centre, sides, low, high, low_step, high_step):
+        for g, (dx, dy) in enumerate(GROUPS):
+            (xa, xb), (ya, yb) = takes[dx], takes[dy]
+            x0, y0 = xa + CX * dx + 2, ya + CY * dy + 2
+            planes, rows = slice(x0, x0 + xb - xa), slice(y0, y0 + yb - ya)
+            for k, c in enumerate(comps):
+                if g == CENTRE:
+                    main[planes, c, rows] = centre[:, c]
+                elif dy == 0:
+                    main[planes, c, rows] = sides(dx, slice(xa, xb), k)
+                elif dy == -1:
+                    first = k * low_step
+                    main[planes, c, rows] = low[dx + 1, xa:xb, first : first + yb - ya]
+                else:
+                    first = k * high_step
+                    main[planes, c, rows] = high[dx + 1, xa:xb, first : first + yb - ya]
+
+    def widened(x, c):
+        turned = pltpu.roll(main[x, c], 2, 1)
+        edge = halo[x, c]
+        head = jnp.where(lane < 2, edge, turned)
+        tail = jnp.where(lane < 2, turned, jnp.where(lane < 5, edge, 0.0))
+        return jnp.concatenate([head, tail], axis=1)
+
+    for dx, dy in around:
+        halo_copy(dx, dy).wait_recv()
+    place(
+        TAKE_BASE, (0, 1, 2), field, lambda dx, planes, k: recv_x[(dx + 1) // 2, planes, k],
+        recv_lo, recv_hi, 1, 2,
+    )
     drain(recv_z_lo.at[0:6], got_z.at[0])
     drain(recv_z_hi.at[0:6], got_z.at[1])
     for g, (dx, dy) in enumerate(GROUPS):
         (xa, xb), (ya, yb) = TAKE[dx], TAKE[dy]
         x0, y0 = xa + CX * dx + 2, ya + CY * dy + 2
-        planes = slice(x0, x0 + xb - xa)
-        if g == CENTRE:
-            main[planes, :, y0 : y0 + CY] = field[...]
-        elif dy == 0:
-            main[planes, :, y0 : y0 + CY] = recv_x[dx == 1 and 1 or 0, xa:xb]
-        else:
-            source, step = (recv_lo, 2) if dy == -1 else (recv_hi, 4)
-            for c in range(4):
-                main[planes, c, y0 : y0 + yb - ya] = source[
-                    dx + 1, xa:xb, c * step : c * step + yb - ya
-                ]
         columns[0:2] = recv_z_lo[g]
         columns[2:6] = recv_z_hi[g]
         ztile[:, :, :, 0:8] = columns[...].T.reshape(CX, 4, CY, 8)
-        halo[planes, :, y0 : y0 + yb - ya] = ztile[xa:xb, :, ya:yb]
-    lane = lax.broadcasted_iota(jnp.int32, (WY, CZ), 1)
-
-    for x in range(WX):
-        for c in range(4):
-            turned = pltpu.roll(main[x, c], 2, 1)
-            edge = halo[x, c]
-            wide[c, x, :, 0:CZ] = jnp.where(lane < 2, edge, turned)
-            wide[c, x, :, CZ:] = jnp.where(lane < 2, turned, jnp.where(lane < 5, edge, 0.0))
-
-    def interpolate():
-        high = vel_h[...].reshape(3 * 11 * WY, WZ)
-        low = vel_l[...].reshape(3 * 11 * WY, WZ)
-        rows = dot3(high, low, own_h[...], own_l[...], ((1,), (0,)))
-        weight = wxy[STARTS[CENTRE] : STARTS[CENTRE] + 11 * WY]
+        halo[x0 : x0 + xb - xa, :, y0 : y0 + yb - ya] = ztile[xa:xb, :, ya:yb]
+
+    def interpolate(planes):
+        first, count = PLACE[planes[0]], len(planes)
+        span = count * WY
+        rows = dot3(
+            vel_h[:, first : first + count].reshape(3 * span, WZ),
+            vel_l[:, first : first + count].reshape(3 * span, WZ),
+            own_h[...], own_l[...], ((1,), (0,)),
+        )
+        starts = [STARTS[CENTRE] + (x - 1) * WY for x in planes]
+        weight = jnp.concatenate([wxy[start : start + WY] for start in starts], axis=0)
         return [
-            jnp.sum(rows[c * 11 * WY : (c + 1) * 11 * WY] * weight, axis=0, keepdims=True)
+            jnp.sum(rows[c * span : (c + 1) * span] * weight, axis=0, keepdims=True)
             for c in range(3)
         ]
 
-    for c in range(3):
-        high, low = split(wide[c, 1:12])
-        vel_h[c] = high
-        vel_l[c] = low
-    for c, value in enumerate(interpolate()):
+    for x in range(1, 12):
+        for c in range(3):
+            high, low = split(widened(x, c))
+            vel_h[c, PLACE[x]] = high
+            vel_l[c, PLACE[x]] = low
+    for c, value in enumerate(interpolate(OUTER + MIDDLE)):
         vecs[0, c : c + 1] = live * (target_ref[c : c + 1] - value)
 
     def send_vector(a):
@@ -330,19 +367,23 @@
         y0, ny = ROWS[dy]
         edges[x0 : x0 + nx, y0 : y0 + ny, 0:32] += spread_edges(a, g).reshape(nx, ny, 32)
 
-    def spread(a):
+    def spread(a, middle):
         far = [abs(dx) + abs(dy) for dx, dy in GROUPS]
         grid[:, :, :, 0:TZ] = jnp.zeros((3, WX, WY, TZ), F32)
         edges[:, :, 0:32] = jnp.zeros((WX, WY, 32), F32)
+        kept = None
         for hops, messages in enumerate((0, 6, 12, 8)):
             if hops:
                 drain(recv_v.at[a, 0:messages], got_v.at[a, hops - 1])
+            if hops == 3:
+                kept = middle()
             for g in range(9):
                 if far[g] == hops:
                     add_inner(a, g)
             for g in range(9):
                 if far[g] == hops - 1:
                     add_edges(a, g)
+        return kept
 
     def shifts(value, axis):
         length = value.shape[axis]
@@ -352,9 +393,9 @@
         before, after = shifts(value, axis)
         return before + after
 
-    def stream(last):
-        for x in range(1, 11) if last else range(WX):
-            scale = wide[3, x]
+    def stream(last, planes, outputs, energy):
+        for x in planes:
+            scale = wide[x]
             edge = edges[x]
             values = []
             for c in range(3):
@@ -388,9 +429,8 @@
             plane_b[2, x] = dz0
             plane_c[1, x] = 2.0 * sz2 + both(sz2, 0) + dyz1
 
-        energy = jnp.zeros((WY, WZ), F32)
-        for x in range(2, 10) if last else range(1, 12):
-            half = wide[3, x] * 0.5
+        for x in outputs:
+            half = wide[x] * 0.5
             for c in range(3):
                 post = plane_a[c, x - 1] + plane_a[c, x + 1] + plane_b[c, x - 1] - plane_b[c, x + 1]
                 if c:
@@ -400,26 +440,28 @@
                     energy = energy + moved[c, x] * response
                 else:
                     high, low = split(half * response)
-                    vel_h[c, x - 1] = high
-                    vel_l[c, x - 1] = low
+                    vel_h[c, PLACE[x]] = high
+                    vel_l[c, PLACE[x]] = low
         return energy
 
     lane_row = lax.broadcasted_iota(jnp.int32, (1, 128), 1)
     me = iy * size_z + iz
     mates = size_y * size_z - 1
+    far_mates = [(y, z) for y in range(size_y) for z in range(size_z) if (y, z) != (0, 0)]
+    far_mates.sort(key=lambda k: -(min(k[0], size_y - k[0]) / 2 + min(k[1], size_z - k[1])))
 
     def sum_plane(k, row):
         part[k] = row
         recv_a[k, me] = row
-        for other in range(1, mates + 1):
-            remote(part.at[k], recv_a.at[k, me], send_r.at[k], got_r.at[k], mate(other)).start()
+        for other in far_mates:
+            remote(part.at[k], recv_a.at[k, me], send_r.at[k], got_r.at[k], mate(*other)).start()
 
     def sum_along(k):
         drain(recv_a.at[k, 0:mates], got_r.at[k])
         row = jnp.sum(recv_a[k], axis=0)
         part_b[k] = row
         recv_b[k, ix] = row
-        for other in range(1, size_x):
+        for other in sorted(range(1, size_x), key=lambda k: -min(k, size_x - k)):
             remote(
                 part_b.at[k], recv_b.at[k, ix], send_r.at[2 + k], got_r.at[2 + k], along(other)
             ).start()
@@ -431,6 +473,14 @@
     for a in range(ITERS):
         send_vector(a)
         if a == 0:
+            for dx, dy in around:
+                scale_copy(dx, dy).wait_recv()
+            place(
+                TAKE, (3,), field, lambda dx, planes, k: srecv_x[(dx + 1) // 2, planes],
+                srecv_lo, srecv_hi, 0, 0,
+            )
+            for x in range(WX):
+                wide[x] = widened(x, 3)
             drain(marks.at[0:26], got_m)
             for g in ORDER:
                 for j in range(3):
@@ -446,14 +496,20 @@
             for k, (left, right) in enumerate(pairs):
                 row = jnp.where(lane_row == k, jnp.sum(left * right), row)
             sum_plane(0, row)
-        spread(a)
+
+        def middle():
+            energy = stream(last, range(4, 9), MIDDLE, jnp.zeros((WY, WZ), F32))
+            return energy if last else interpolate(MIDDLE)
+
+        kept = spread(a, middle)
         if last:
             sum_along(0)
-        energy = stream(last)
-        if not last:
-            for c, value in enumerate(interpolate()):
+            energy = stream(last, (1, 2, 3, 9, 10), (2, 3, 4, 8, 9), kept)
+        else:
+            stream(last, (0, 1, 2, 3, 9, 10, 11, 12), OUTER, None)
+            for c, value in enumerate(interpolate(OUTER)):
                 vector = vecs[a, c : c + 1]
-                image = live * (value + stiff * vector)
+                image = live * (kept[c] + value + stiff * vector)
                 images[a, c : c + 1] = image
                 vecs[a + 1, c : c + 1] = image - SHIFT * vector
 
@@ -492,6 +548,7 @@
     for dx, dy in GROUPS:
         if (dx, dy) != (0, 0):
             halo_copy(dx, dy).wait_send()
+            scale_copy(dx, dy).wait_send()
     drain(recv_z_lo.at[0:6], send_z.at[0])
     drain(recv_z_hi.at[0:6], send_z.at[1])
     drain(marks.at[0:26], send_m)
@@ -522,14 +579,19 @@
                 pltpu.VMEM((1, CAP), F32),
                 pltpu.VMEM((CX, 4, CY, CZ), F32),
                 pltpu.VMEM((CZ, 4 * CX * CY), F32),
+                pltpu.VMEM((CX, 4, CZ), F32),
                 pltpu.VMEM((CX, 8, CZ), F32),
-                pltpu.VMEM((CX, 16, CZ), F32),
+                pltpu.VMEM((CX, 2, CZ), F32),
+                pltpu.VMEM((CX, 4, CZ), F32),
                 pltpu.VMEM((2, 4 * CX * CY), F32),
                 pltpu.VMEM((4, 4 * CX * CY), F32),
                 pltpu.VMEM((8, CAP), F32),
-                pltpu.VMEM((2, CX, 4, CY, CZ), F32),
+                pltpu.VMEM((2, CX, 3, CY, CZ), F32),
+                pltpu.VMEM((3, CX, 4, CZ), F32),
                 pltpu.VMEM((3, CX, 8, CZ), F32),
-                pltpu.VMEM((3, CX, 16, CZ), F32),
+                pltpu.VMEM((2, CX, CY, CZ), F32),
+                pltpu.VMEM((3, CX, 2, CZ), F32),
+                pltpu.VMEM((3, CX, 4, CZ), F32),
                 pltpu.VMEM((9, 2, 4 * CX * CY), F32),
                 pltpu.VMEM((9, 4, 4 * CX * CY), F32),
                 pltpu.VMEM((8, 4 * CX * CY), F32),
@@ -537,7 +599,7 @@
                 pltpu.VMEM((WX, 4, WY, CZ), F32),
                 pltpu.VMEM((WX, 4, WY, CZ), F32),
                 pltpu.VMEM((CX, 4, CY, CZ), F32),
-                pltpu.VMEM((4, WX, WY, WZ), F32),
+                pltpu.VMEM((WX, WY, WZ), F32),
                 pltpu.VMEM((9, TZ, CAP), BF16),
                 pltpu.VMEM((9, TZ, CAP), BF16),
                 pltpu.VMEM((WZ, CAP), BF16),
@@ -566,6 +628,8 @@
                 pltpu.SemaphoreType.DMA((9,)),
                 pltpu.SemaphoreType.DMA((9,)),
                 pltpu.SemaphoreType.DMA((9,)),
+                pltpu.SemaphoreType.DMA((9,)),
+                pltpu.SemaphoreType.DMA((9,)),
                 pltpu.SemaphoreType.DMA((2,)),
                 pltpu.SemaphoreType.DMA((2,)),
                 pltpu.SemaphoreType.DMA,

time: 48.7 us -> 47.1 us (0.967)
  Pallas kernels: 46.6 us -> 45.1 us
    pallas_call x1, Pallas kernels: 46.6 us -> 45.1 us  [body(): pl.pallas_call(functools.partial(kernel, sizes), out_shape=jax.ShapeDtype...]
where the time goes in v4:
time: 47.1 us; the launch traced here: 47 us
  Pallas kernels  45.1 us (96%)
  local copies, waits for them, and re-layouts  1.28 us (3%)
  between operations  0.66 us (1%)
    pallas_call x1, Pallas kernels, body(): pl.pallas_call(functools.partial(kernel, sizes), out_shape=jax.ShapeDtype...  45.1 us
    unnamed x1, local copies, waits for them, and re-layouts  1.28 us

profile of v4, /device:TPU:1, one launch (start us, length us, event | category | flops | bytes accessed | tf_op | source)
XLA Modules:
  0.0 47.0 jit_solution(10175530178969518022)
XLA Ops:
  0.7 45.1 %immersed.1 = f32[3,256]{1,0:T(4,128)} custom-call(f32[8,8,128]{2,1,0:T(8,128)} %density_in.1, f32[3,8,8,128]{3,2,1,0:T(8,128)} %base_in.1, s32[3,256]{1,0:T(4,128)} %cells_in.1, f32[3,256]{1,0:T(4,128)} %offsets_in.1, f32[3,256]{1,0:T(4,128)} %target_in.1, f32[1,256]{1,0:T(1,128)} %bitcast.1, s32[1]{0:T(128)S(6)} %copy.9.counts_in), custom_call_target="tpu_custom_call" | custom-call | tf_op jit(solution)/shard_map/immersed/pallas_call | solution.py:568
  45.7 1.3 %copy.10 = f32[3,256]{1,0:T(4,128)} copy(f32[3,256]{1,0:T(4,128)} %immersed.1) | data formatting | bytes 6144

commit v5 on v4

--- a/solution.py
+++ b/solution.py
@@ -59,7 +59,9 @@
     dot = functools.partial(
         lax.dot_general, dimension_numbers=(dims, ((), ())), preferred_element_type=F32
     )
-    return dot(lh, rh) + (dot(ll, rh) + dot(lh, rl))
+    count = lh.shape[0]
+    both = dot(jnp.concatenate([lh, ll], axis=0), rh)
+    return both[:count] + (both[count:] + dot(lh, rl))
 
 
 def kernel(
@@ -109,15 +111,6 @@
     barrier = pltpu.get_barrier_semaphore()
     for offset in NEIGHBOURS:
         pl.semaphore_signal(barrier, inc=1, device_id=at(*offset), device_id_type=MESH)
-
-    def greet_mate(k, carry):
-        other = mate(k // size_z, lax.rem(k, size_z))
-        pl.semaphore_signal(barrier, inc=1, device_id=other, device_id_type=MESH)
-        return carry
-
-    lax.fori_loop(1, size_y * size_z, greet_mate, 0)
-    for k in range(1, size_x):
-        pl.semaphore_signal(barrier, inc=1, device_id=along(k), device_id_type=MESH)
 
     for load in loads:
         load.wait()
@@ -137,7 +130,7 @@
     mark_own[6:8] = jnp.zeros((2, CAP), F32)
     marks[slot_of(0, 0, 0)] = mark_own[...]
 
-    pl.semaphore_wait(barrier, len(NEIGHBOURS) + size_y * size_z - 1 + size_x - 1)
+    pl.semaphore_wait(barrier, len(NEIGHBOURS))
 
     def remote(src, dst, send, recv, device):
         return pltpu.make_async_remote_copy(
@@ -394,6 +387,7 @@
         return before + after
 
     def stream(last, planes, outputs, energy):
+        inner = range(2, 10) if last else range(1, 12)
         for x in planes:
             scale = wide[x]
             edge = edges[x]
@@ -416,18 +410,17 @@
             sz0, dz0 = before + after, before - after
             before, after = shifts(m2, 1)
             sz2, dz2 = before + after, before - after
-            before, after = shifts(dz2, 0)
-            dyz2 = before - after
-            before, after = shifts(dy1, 1)
-            dyz1 = before - after
             plane_a[0, x] = 2.0 * m0 + sy0 + sz0
             plane_b[0, x] = dy1 + dz2
             plane_a[1, x] = sy1
             plane_b[1, x] = dy0
-            plane_c[0, x] = 2.0 * sy1 + both(sy1, 1) + dyz2
             plane_a[2, x] = sz2
             plane_b[2, x] = dz0
-            plane_c[1, x] = 2.0 * sz2 + both(sz2, 0) + dyz1
+            if x in inner:
+                before, after = shifts(dz2, 0)
+                plane_c[0, x] = 2.0 * sy1 + both(sy1, 1) + (before - after)
+                before, after = shifts(dy1, 1)
+                plane_c[1, x] = 2.0 * sz2 + both(sz2, 0) + (before - after)
 
         for x in outputs:
             half = wide[x] * 0.5

time: 47.1 us -> 46.4 us (0.985)
  Pallas kernels: 45.1 us -> 44.2 us
    pallas_call x1, Pallas kernels: 45.1 us -> 44.2 us  [body(): pl.pallas_call(functools.partial(kernel, sizes), out_shape=jax.ShapeDtype...]
where the time goes in v5:
time: 46.4 us; the launch traced here: 46.1 us
  Pallas kernels  44.2 us (95%)
  local copies, waits for them, and re-layouts  1.28 us (3%)
  between operations  0.66 us (1%)
    pallas_call x1, Pallas kernels, body(): pl.pallas_call(functools.partial(kernel, sizes), out_shape=jax.ShapeDtype...  44.2 us
    unnamed x1, local copies, waits for them, and re-layouts  1.28 us

profile of v5, /device:TPU:1, one launch (start us, length us, event | category | flops | bytes accessed | tf_op | source)
XLA Modules:
  0.0 46.1 jit_solution(16708736633990522293)
XLA Ops:
  0.7 44.2 %immersed.1 = f32[3,256]{1,0:T(4,128)} custom-call(f32[8,8,128]{2,1,0:T(8,128)} %density_in.1, f32[3,8,8,128]{3,2,1,0:T(8,128)} %base_in.1, s32[3,256]{1,0:T(4,128)} %cells_in.1, f32[3,256]{1,0:T(4,128)} %offsets_in.1, f32[3,256]{1,0:T(4,128)} %target_in.1, f32[1,256]{1,0:T(1,128)} %bitcast.1, s32[1]{0:T(128)S(6)} %copy.9.counts_in), custom_call_target="tpu_custom_call" | custom-call | tf_op jit(solution)/shard_map/immersed/pallas_call | solution.py:561
  44.9 1.3 %copy.10 = f32[3,256]{1,0:T(4,128)} copy(f32[3,256]{1,0:T(4,128)} %immersed.1) | data formatting | bytes 6144

commit v6 on v5

--- a/solution.py
+++ b/solution.py
@@ -109,10 +109,10 @@
         load.start()
 
     barrier = pltpu.get_barrier_semaphore()
-    for offset in NEIGHBOURS:
+    for offset in reversed(NEIGHBOURS):
         pl.semaphore_signal(barrier, inc=1, device_id=at(*offset), device_id_type=MESH)
 
-    for load in loads:
+    for load in loads[0:4]:
         load.wait()
     field[:, 3] = lax.rsqrt(density_ref[...])
     ftrans[...] = field[...].reshape(4 * CX * CY, CZ).T
@@ -123,6 +123,8 @@
         pack_hi[:, 2 * c : 2 * c + 2] = field[:, c, 0:2]
     spack_lo[...] = field[:, 3, CY - 2 : CY]
     spack_hi[...] = field[:, 3, 0:4]
+    for load in loads[4:]:
+        load.wait()
     anchors = (ix * CX, iy * CY, iz * CZ)
     for k in range(3):
         mark_own[k : k + 1] = (cells_ref[k : k + 1] - anchors[k]).astype(F32)
@@ -491,18 +493,17 @@
             sum_plane(0, row)
 
         def middle():
-            energy = stream(last, range(4, 9), MIDDLE, jnp.zeros((WY, WZ), F32))
-            return energy if last else interpolate(MIDDLE)
+            return None
 
         kept = spread(a, middle)
         if last:
             sum_along(0)
-            energy = stream(last, (1, 2, 3, 9, 10), (2, 3, 4, 8, 9), kept)
+            energy = stream(last, range(1, 11), range(2, 10), jnp.zeros((WY, WZ), F32))
         else:
-            stream(last, (0, 1, 2, 3, 9, 10, 11, 12), OUTER, None)
-            for c, value in enumerate(interpolate(OUTER)):
+            stream(last, range(WX), range(1, 12), None)
+            for c, value in enumerate(interpolate(OUTER + MIDDLE)):
                 vector = vecs[a, c : c + 1]
-                image = live * (kept[c] + value + stiff * vector)
+                image = live * (value + stiff * vector)
                 images[a, c : c + 1] = image
                 vecs[a + 1, c : c + 1] = image - SHIFT * vector
 

time: 46.4 us -> 46.6 us (level)
  no operation moved by 1% of the time
where the time goes in v6:
time: 46.6 us; the launch traced here: 46.4 us
  Pallas kernels  44.4 us (95%)
  local copies, waits for them, and re-layouts  1.28 us (3%)
  between operations  0.66 us (1%)
    pallas_call x1, Pallas kernels, body(): pl.pallas_call(functools.partial(kernel, sizes), out_shape=jax.ShapeDtype...  44.4 us
    unnamed x1, local copies, waits for them, and re-layouts  1.28 us

profile of v6, /device:TPU:1, one launch (start us, length us, event | category | flops | bytes accessed | tf_op | source)
XLA Modules:
  0.0 46.4 jit_solution(6095667152834329749)
XLA Ops:
  0.7 44.4 %immersed.1 = f32[3,256]{1,0:T(4,128)} custom-call(f32[8,8,128]{2,1,0:T(8,128)} %density_in.1, f32[3,8,8,128]{3,2,1,0:T(8,128)} %base_in.1, s32[3,256]{1,0:T(4,128)} %cells_in.1, f32[3,256]{1,0:T(4,128)} %offsets_in.1, f32[3,256]{1,0:T(4,128)} %target_in.1, f32[1,256]{1,0:T(1,128)} %bitcast.1, s32[1]{0:T(128)S(6)} %copy.9.counts_in), custom_call_target="tpu_custom_call" | custom-call | tf_op jit(solution)/shard_map/immersed/pallas_call | solution.py:562
  45.1 1.3 %copy.10 = f32[3,256]{1,0:T(4,128)} copy(f32[3,256]{1,0:T(4,128)} %immersed.1) | data formatting | bytes 6144

commit v7 on v6

--- a/solution.py
+++ b/solution.py
@@ -112,7 +112,7 @@
     for offset in reversed(NEIGHBOURS):
         pl.semaphore_signal(barrier, inc=1, device_id=at(*offset), device_id_type=MESH)
 
-    for load in loads[0:4]:
+    for load in loads:
         load.wait()
     field[:, 3] = lax.rsqrt(density_ref[...])
     ftrans[...] = field[...].reshape(4 * CX * CY, CZ).T
@@ -123,8 +123,6 @@
         pack_hi[:, 2 * c : 2 * c + 2] = field[:, c, 0:2]
     spack_lo[...] = field[:, 3, CY - 2 : CY]
     spack_hi[...] = field[:, 3, 0:4]
-    for load in loads[4:]:
-        load.wait()
     anchors = (ix * CX, iy * CY, iz * CZ)
     for k in range(3):
         mark_own[k : k + 1] = (cells_ref[k : k + 1] - anchors[k]).astype(F32)
@@ -175,7 +173,7 @@
         side = (1 - dz) // 2
         return remote(*pair, send_z.at[side], got_z.at[side], at(dx, dy, dz))
 
-    around = [GROUPS[g] for g in reversed(ORDER) if g != CENTRE]
+    around = [GROUPS[g] for g in ORDER if g != CENTRE]
     for dx, dy, dz in NEIGHBOURS:
         if dz:
             edge_copy(dx, dy, dz).start()

time: 46.6 us -> 46.6 us (level)
  no operation moved by 1% of the time
where the time goes in v7:
time: 46.6 us; the launch traced here: 46.4 us
  Pallas kernels  44.4 us (95%)
  local copies, waits for them, and re-layouts  1.28 us (3%)
  between operations  0.66 us (1%)
    pallas_call x1, Pallas kernels, body(): pl.pallas_call(functools.partial(kernel, sizes), out_shape=jax.ShapeDtype...  44.4 us
    unnamed x1, local copies, waits for them, and re-layouts  1.28 us

profile of v7, /device:TPU:1, one launch (start us, length us, event | category | flops | bytes accessed | tf_op | source)
XLA Modules:
  0.0 46.4 jit_solution(7346980036777690474)
XLA Ops:
  0.7 44.4 %immersed.1 = f32[3,256]{1,0:T(4,128)} custom-call(f32[8,8,128]{2,1,0:T(8,128)} %density_in.1, f32[3,8,8,128]{3,2,1,0:T(8,128)} %base_in.1, s32[3,256]{1,0:T(4,128)} %cells_in.1, f32[3,256]{1,0:T(4,128)} %offsets_in.1, f32[3,256]{1,0:T(4,128)} %target_in.1, f32[1,256]{1,0:T(1,128)} %bitcast.1, s32[1]{0:T(128)S(6)} %copy.9.counts_in), custom_call_target="tpu_custom_call" | custom-call | tf_op jit(solution)/shard_map/immersed/pallas_call | solution.py:560
  45.1 1.3 %copy.10 = f32[3,256]{1,0:T(4,128)} copy(f32[3,256]{1,0:T(4,128)} %immersed.1) | data formatting | bytes 6144
